TPU v7x, 256 devices: a whole 4x4x8 slice. The times are simulated.
256 devices in a mesh: replica: 8 (over y, core), shard: 32 (over x, z).
Axes of the slice: x: 4, y: 4, z: 8, core: 2. Of those that a mesh axis runs over, the one named last changes fastest.
Arguments:
- deltas: bfloat16 [8, 64, 128, 6144], P('replica', None, 'shard')
- block_list: int32 [8, 64], replicated, may hold values from -1 to 127, as said below
- hosting: int32 [8, 16, 8], replicated, may hold values from 0 to 1, as said below
- counts: int32 [8, 128], replicated, may hold values from 1 to 63
- params: float32 [128, 128, 6144], P('shard', 'replica'), may hold values from -6 to 6
- momentum: float32 [128, 128, 6144], P('shard', 'replica'), may hold values from -4 to 4
Outputs:
- new_params: float32 [128, 128, 6144], P('shard', 'replica')
- new_momentum: float32 [128, 128, 6144], P('shard', 'replica')
- host_params: bfloat16 [8, 64, 128, 6144], P('replica', None, 'shard')
Inputs may be any that keep to these rules, and one draw needn't show every extreme that they name: `block_list`: row r lists, each once and in any order, the blocks whose parameters replica r holds, with -1 in the other entries; block b is owned by shard b // 4, and at most 2 listed blocks of one row have the same owner. `hosting`: 1 only for blocks that appear in the replica's row of block_list.
All inputs are finite; a program needn't handle non-finite values.
Results may differ from a plain program's by a relative error of at most 0.001.
Values may be sent and summed in bfloat16 or wider, within the bound.
A program may use at most 128 MiB of HBM per device.

v0:
```python
import math

import jax
import jax.numpy as jnp
from jax import lax
from jax.sharding import Mesh
from jax.sharding import PartitionSpec as P

D = 6144
ROWS = 128
REPLICA = ("replica_0", "replica_1")
SHARD = ("shard_0", "shard_1")
REPLICA_SHARD = ("replica_0", "replica_1", "shard_0", "shard_1")


decay_rate = 0.9
outer_rate = 0.7
limit_ratio = 0.1


def by_axis(shard, axes):
    for axis in axes:
        shard = lax.psum(shard, axis)
    return shard


def slot_placement(block_lists, owned_count, capacity, shard_count):
    listed = block_lists >= 0
    owner_shard = jnp.where(listed, block_lists // owned_count, -1)
    same_owner = (owner_shard[:, :, None] == jnp.arange(shard_count)[None, None, :]).astype(
        jnp.int32
    )
    owner_rank = jnp.sum(jnp.cumsum(same_owner, axis=1) * same_owner, axis=2) - 1
    return jnp.where(listed, owner_shard * capacity + owner_rank, -1)


def per_device(deltas, block_list, hosting, counts, params, momentum):
    replicas = lax.axis_size(REPLICA)
    shard_count = lax.axis_size(SHARD)
    replica_index = lax.axis_index(REPLICA)
    shard_index = lax.axis_index(SHARD)
    slot_count = block_list.shape[1]
    capacity = slot_count // shard_count
    block_count = counts.shape[1]
    owned_count = block_count // shard_count
    local_rows = deltas.shape[2]
    owner_rows = params.shape[1]
    flat_local = deltas[0].reshape(slot_count, local_rows * D)
    weight = hosting.reshape(replicas, block_count) * counts
    totals = jnp.maximum(jnp.sum(weight, axis=0).astype(jnp.float32), 1.0)
    first_owned = shard_index * owned_count
    targets = first_owned + jnp.arange(owned_count)
    own_weight = lax.dynamic_slice_in_dim(weight, first_owned, owned_count, 1)
    own_totals = lax.dynamic_slice_in_dim(totals, first_owned, owned_count, 0)
    placement_all = slot_placement(block_list, owned_count, capacity, shard_count)
    my_place = lax.dynamic_index_in_dim(placement_all, replica_index, 0, keepdims=False)
    packing = (jnp.arange(slot_count)[:, None] == my_place[None, :]).astype(jnp.bfloat16)
    packed = jnp.dot(packing, flat_local, preferred_element_type=jnp.float32).astype(jnp.bfloat16)
    packed = packed.reshape(shard_count, capacity, local_rows, D)
    at_owner = lax.all_to_all(packed, SHARD, split_axis=0, concat_axis=2, tiled=True)
    gathered = lax.all_to_all(at_owner, REPLICA, split_axis=2, concat_axis=0, tiled=True)
    wanted = shard_index * capacity + jnp.arange(capacity)
    select = (placement_all[:, None, :] == wanted[None, :, None]).astype(jnp.int32)
    slot_block = jnp.sum(select * block_list[:, None, :], axis=2) - (1 - jnp.sum(select, axis=2))
    matches = slot_block[:, :, None] == targets[None, None, :]
    slot_weight = jnp.where(matches, own_weight[:, None, :], 0)
    mixing = slot_weight.reshape(replicas * capacity, owned_count).astype(jnp.bfloat16)
    summed = jnp.einsum(
        "sj,sx->jx",
        mixing,
        gathered.reshape(replicas * capacity, owner_rows * D),
        preferred_element_type=jnp.float32,
    )
    gradient = summed.reshape(owned_count, owner_rows, D) / own_totals[:, None, None]
    square_sum = by_axis(jnp.sum(gradient * gradient), REPLICA_SHARD)
    limit = limit_ratio * math.sqrt(block_count * ROWS * D)
    clip_factor = jnp.minimum(1.0, limit / jnp.sqrt(square_sum + 1e-06))
    scaled = clip_factor * gradient
    new_momentum = decay_rate * momentum + scaled
    new_params = params - outer_rate * (scaled + decay_rate * new_momentum)
    hosted = new_params.astype(jnp.bfloat16)
    sending = jnp.einsum(
        "rcj,jx->rcx",
        matches.astype(jnp.bfloat16),
        hosted.reshape(owned_count, owner_rows * D),
        preferred_element_type=jnp.float32,
    ).astype(jnp.bfloat16)
    sending = sending.reshape(replicas, capacity, owner_rows, D)
    returned = lax.all_to_all(
        lax.all_to_all(sending, REPLICA, split_axis=0, concat_axis=2, tiled=True),
        SHARD,
        split_axis=2,
        concat_axis=0,
        tiled=True,
    )
    host_rows = jnp.einsum(
        "pk,px->kx",
        packing,
        returned.reshape(slot_count, local_rows * D),
        preferred_element_type=jnp.float32,
    ).astype(jnp.bfloat16)
    return (new_params, new_momentum, host_rows.reshape(1, slot_count, local_rows, D))


def solution(mesh):
    finer = Mesh(mesh.devices.reshape(4, 2, 4, 8), ("replica_0", "replica_1", "shard_0", "shard_1"))
    in_specs = (
        P(REPLICA, None, SHARD, None),
        P(),
        P(),
        P(),
        P(SHARD, REPLICA, None),
        P(SHARD, REPLICA, None),
    )
    out_specs = (P(SHARD, REPLICA, None), P(SHARD, REPLICA, None), P(REPLICA, None, SHARD, None))
    return jax.shard_map(
        per_device, mesh=finer, in_specs=in_specs, out_specs=out_specs, check_vma=False
    )
```

profile of v0, /device:TPU:1, one launch (start us, length us, event | category | flops | bytes accessed | tf_op | source)
XLA Modules:
  0.0 329.5 jit_solution(15116666798434059264)
XLA Ops:
  0.6 0.8 copy.72
  1.4 1.3 fusion.15
  2.8 3.7 %copy.97 = bf16[8,8,4,6144]{3,1,2,0:T(8,128)(2,1)S(1)} copy(bf16[8,8,4,6144]{3,2,1,0:T(4,128)(2,1)} %bitcast.58) | data formatting | bytes 6291456
  6.5 0.2 dynamic-slice_reduce_fusion
  6.7 2.6 convolution_convert_fusion.2
  9.3 4.1 %reshape.102 = bf16[32,2,4,6144]{3,2,1,0:T(4,128)(2,1)S(1)} reshape(bf16[64,24576]{1,0:T(8,128)(2,1)} %convolution_convert_fusion.2) | data formatting | bytes 6291456 | tf_op jit(solution)/shard_map/reshape | solution.py:59
  13.4 3.2 copy.80
  16.7 81.2 %all_to_all.66 = bf16[32,2,4,6144]{3,1,2,0:T(2,128)(2,1)} all-to-all(bf16[32,2,4,6144]{3,1,2,0:T(2,128)(2,1)S(1)} %copy.80), channel_id=1, replica_groups=mesh['replica_0'=4,'replica_1'=2,'shard_0'=4,'shard_1'=8] {'shard_0','sh..., dimensions={0} | all-to-all | bytes 6291456 | tf_op jit(solution)/shard_map/all_to_all | solution.py:60
  97.9 9.7 %all-to-all-start.1 = ((bf16[1,2,128,6144]{3,1,0,2:T(2,128)(2,1)}), bf16[1,2,128,6144]{3,1,0,2:T(2,128)(2,1)S(1)}, u32[]{:S(2)}, u32[]{:S(2)}) async-start(bf16[1,2,128,6144]{3,1,0,2:T(2,128)(2,1)} %bitcast.50), calls=%async_computation.1 | async-start | bytes 6291456 | tf_op jit(solution)/shard_map/all_to_all | solution.py:61
  107.7 0.2 fusion.11
  108.1 0.1 reshape.101
  108.5 36.6 %all-to-all-done.1 = bf16[1,2,128,6144]{3,1,0,2:T(2,128)(2,1)S(1)} async-done(((bf16[1,2,128,6144]{3,1,0,2:T(2,128)(2,1)}), bf16[1,2,128,6144]{3,1,0,2:T(2,128)(2,1)S(1)}, u32[]{:S(2)}, u32[]{:S(2)}) %all-to-all-start.1) | async-done | bytes 3145760 | tf_op jit(solution)/shard_map/all_to_all | solution.py:61
  145.1 1.1 copy.82
  146.2 5.2 %multiply_reduce_fusion = (f32[]{:T(128)}, f32[4,16,6144]{2,0,1:T(4,128)}) fusion(f32[4]{0:T(128)S(1)} %dynamic_slice.12, bf16[16,4,1]{1,0,2:T(8,128)(2,1)S(1)} %bitcast.60, bf16[2,8,16,6144]{3,2,1,0:T(8,128)(2,1)S(1)} %bitcast.59), kind=kOutput, calls=%fused_computation.9 | convolution fusion | flops 13762559 | bytes 4718740 | tf_op jit(solution)/shard_map/sj,sx->jx/dot_general | solution.py:68
  151.4 7.5 %psum.28 = f32[]{:T(128)} all-reduce(f32[]{:T(128)} %get-tuple-element.27), channel_id=1, replica_groups=mesh['replica_0'=4,'replica_1'=2,'shard_0'=4,'shard_1'=8] {'replica_0'}, use_global_device_ids=true, to_apply=%region_6.7 | all-reduce | flops 1 | bytes 8 | tf_op jit(solution)/shard_map/psum | solution.py:23
  158.9 5.7 %psum.29 = f32[]{:T(128)} all-reduce(f32[]{:T(128)} %psum.28), channel_id=1, replica_groups=mesh['replica_0'=4,'replica_1'=2,'shard_0'=4,'shard_1'=8] {'replica_1'}, use_global_device_ids=true, to_apply=%region_7.8 | all-reduce | flops 1 | bytes 8 | tf_op jit(solution)/shard_map/psum | solution.py:23
  164.6 7.1 %psum.30 = f32[]{:T(128)} all-reduce(f32[]{:T(128)} %psum.29), channel_id=1, replica_groups=mesh['replica_0'=4,'replica_1'=2,'shard_0'=4,'shard_1'=8] {'shard_0'}, use_global_device_ids=true, to_apply=%region_8.9 | all-reduce | flops 1 | bytes 8 | tf_op jit(solution)/shard_map/psum | solution.py:23
  171.7 13.1 %psum.31 = f32[]{:T(128)} all-reduce(f32[]{:T(128)} %psum.30), channel_id=1, replica_groups=mesh['replica_0'=4,'replica_1'=2,'shard_0'=4,'shard_1'=8] {'shard_1'}, use_global_device_ids=true, to_apply=%region_9.10 | all-reduce | flops 1 | bytes 8 | tf_op jit(solution)/shard_map/psum | solution.py:23
  185.5 6.0 %fusion.13 = (bf16[4,16,6144]{2,0,1:T(4,128)(2,1)S(1)}, f32[4,16,6144]{2,0,1:T(4,128)}, f32[4,16,6144]{2,0,1:T(4,128)}) fusion(f32[4,16,6144]{2,1,0:T(8,128)S(1)} %copy-done.1, f32[4,16,6144]{2,0,1:T(4,128)} %get-tuple-element.28, f32[]{:T(128)S(6)} %min.3, f32[4,16,6144]{2,1,0:T(8,128)S(1)} %copy-done.2), kind=kLoop, calls=%fused_computation.40 | loop fusion | flops 3145728 | bytes 8650756 | tf_op jit(solution)/shard_map/convert_element_type | solution.py:81
  191.4 1.0 convolution_convert_fusion
  192.4 1.7 copy.88
  194.1 46.0 %all_to_all.67 = bf16[8,2,16,6144]{3,2,1,0:T(8,128)(2,1)S(1)} all-to-all(bf16[8,2,16,6144]{3,2,1,0:T(8,128)(2,1)S(1)} %copy.88), channel_id=1, replica_groups=mesh['replica_0'=4,'replica_1'=2,'shard_0'=4,'shard_1'=8] {'replica_0','..., dimensions={0} | all-to-all | bytes 6291456 | tf_op jit(solution)/shard_map/all_to_all | solution.py:90
  240.1 0.2 copy.89
  240.3 4.9 %copy.90 = bf16[1,2,128,6144]{3,1,0,2:T(2,128)(2,1)} copy(bf16[1,2,128,6144]{3,2,1,0:T(8,128)(2,1)S(1)} %bitcast.55) | data formatting | bytes 6291456 | tf_op jit(solution)/shard_map/all_to_all | solution.py:90
  245.2 5.0 %all-to-all-start.3 = ((bf16[1,2,128,6144]{3,1,0,2:T(2,128)(2,1)}), bf16[1,2,128,6144]{3,1,0,2:T(2,128)(2,1)S(1)}, u32[]{:S(2)}, u32[]{:S(2)}) async-start(bf16[1,2,128,6144]{3,1,0,2:T(2,128)(2,1)} %copy.90), calls=%async_computation.3 | async-start | bytes 6291456 | tf_op jit(solution)/shard_map/all_to_all | solution.py:89
  250.3 3.6 %copy.92 = f32[4,16,6144]{2,1,0:T(8,128)} copy(f32[4,16,6144]{2,0,1:T(4,128)} %get-tuple-element.21) | data formatting | bytes 3145728
  253.9 2.1 copy.93
  255.9 65.6 %all-to-all-done.3 = bf16[1,2,128,6144]{3,1,0,2:T(2,128)(2,1)S(1)} async-done(((bf16[1,2,128,6144]{3,1,0,2:T(2,128)(2,1)}), bf16[1,2,128,6144]{3,1,0,2:T(2,128)(2,1)S(1)}, u32[]{:S(2)}, u32[]{:S(2)}) %all-to-all-start.3) | async-done | bytes 3145760 | tf_op jit(solution)/shard_map/all_to_all | solution.py:89
  321.5 1.6 copy.91
  323.1 1.8 copy.99
  324.9 1.0 convolution_convert_fusion.1
  325.9 3.6 %reshape.107 = bf16[1,64,4,6144]{3,2,1,0:T(4,128)(2,1)} reshape(bf16[64,24576]{1,0:T(8,128)(2,1)S(1)} %convolution_convert_fusion.1) | data formatting | bytes 6291456 | tf_op jit(solution)/shard_map/reshape | solution.py:102
  (25 shorter events, 0.6 us)
Async XLA Ops:
  97.9 9.8 %copy-start.4 = (s32[8,64]{1,0:T(8,128)S(1)}, s32[8,64]{1,0:T(8,128)}, u32[]{:S(2)}) copy-start(s32[8,64]{1,0:T(8,128)} %param.7) | copy-start | bytes 6148
  97.9 10.1 %copy-start.3 = (s32[8,16,8]{1,2,0:T(8,128)S(1)}, s32[8,16,8]{1,2,0:T(8,128)}, u32[]{:S(2)}) copy-start(s32[8,16,8]{1,2,0:T(8,128)} %param.8) | copy-start | bytes 12292
  97.9 10.3 %copy-start.5 = (s32[8,128]{1,0:T(8,128)S(1)}, s32[8,128]{1,0:T(8,128)}, u32[]{:S(2)}) copy-start(s32[8,128]{1,0:T(8,128)} %param.9) | copy-start | bytes 12292
  97.9 47.2 %all-to-all-start.1 = ((bf16[1,2,128,6144]{3,1,0,2:T(2,128)(2,1)}), bf16[1,2,128,6144]{3,1,0,2:T(2,128)(2,1)S(1)}, u32[]{:S(2)}, u32[]{:S(2)}) async-start(bf16[1,2,128,6144]{3,1,0,2:T(2,128)(2,1)} %bitcast.50), calls=%async_computation.1 | async-start | bytes 6291456 | tf_op jit(solution)/shard_map/all_to_all | solution.py:61
  146.2 39.3 %copy-start.1 = (f32[4,16,6144]{2,1,0:T(8,128)S(1)}, f32[4,16,6144]{2,1,0:T(8,128)}, u32[]{:S(2)}) copy-start(f32[4,16,6144]{2,1,0:T(8,128)} %param.11) | copy-start | bytes 4718596
  146.2 39.3 %copy-start.2 = (f32[4,16,6144]{2,1,0:T(8,128)S(1)}, f32[4,16,6144]{2,1,0:T(8,128)}, u32[]{:S(2)}) copy-start(f32[4,16,6144]{2,1,0:T(8,128)} %param.10) | copy-start | bytes 4718596
  245.2 76.2 %all-to-all-start.3 = ((bf16[1,2,128,6144]{3,1,0,2:T(2,128)(2,1)}), bf16[1,2,128,6144]{3,1,0,2:T(2,128)(2,1)S(1)}, u32[]{:S(2)}, u32[]{:S(2)}) async-start(bf16[1,2,128,6144]{3,1,0,2:T(2,128)(2,1)} %copy.90), calls=%async_computation.3 | async-start | bytes 6291456 | tf_op jit(solution)/shard_map/all_to_all | solution.py:89
  250.3 3.6 %copy-start = (f32[4,16,6144]{2,0,1:T(4,128)S(1)}, f32[4,16,6144]{2,0,1:T(4,128)}, u32[]{:S(2)}) copy-start(f32[4,16,6144]{2,0,1:T(4,128)} %get-tuple-element.26) | copy-start | bytes 4718596
where the time goes:
time: 332 us; the launch traced here: 330 us
  blocking collectives  161 us (48%)
  waiting for transfers between devices  102 us (31%)
  local copies, waits for them, and re-layouts  33.1 us (10%)
  starting transfers between devices  14.8 us (4%)
  matrix products  9.8 us (3%)
  other arithmetic  7.66 us (2%)
    all_to_all x1, blocking collectives, per_device(): lax.all_to_all(packed, SHARD, split_axis=0, concat_axis=2, tiled=True)  81.2 us
    all_to_all x1, waiting for transfers between devices, per_device(): lax.all_to_all(lax.all_to_all(sending, REPLICA, split_axis=0, concat_axis...  65.6 us
    all_to_all x1, blocking collectives, per_device(): lax.all_to_all(sending, REPLICA, split_axis=0, concat_axis=2, tiled=True)  46 us
    all_to_all x1, waiting for transfers between devices, per_device(): lax.all_to_all(at_owner, REPLICA, split_axis=2, concat_axis=0, tiled=True)  36.6 us
    psum x4, blocking collectives, by_axis(): shard = lax.psum(shard, axis)  33.4 us
    unnamed x18, local copies, waits for them, and re-layouts  12 us
    all_to_all x1, starting transfers between devices, per_device(): lax.all_to_all(at_owner, REPLICA, split_axis=2, concat_axis=0, tiled=True)  9.73 us
    reshape x2, local copies, waits for them, and re-layouts, per_device(): packed = packed.reshape(shard_count, capacity, local_rows, D)  7.37 us
  transfers between devices with their start and end apart: 2, of which 2 were waited for; matrix products, arithmetic and copies ran while one was open for 2% of the time, Pallas kernels for 0%

commit v1 on v0

v1 whole, which is shorter than its diff:
```python
import functools
import math

import jax
import jax.numpy as jnp
from jax import lax
from jax.experimental import pallas as pl
from jax.experimental.pallas import tpu as pltpu
from jax.sharding import PartitionSpec as P

D = 6144
ROWS = 128
HALF = D // 2
CHUNKS = 4
DC = HALF // CHUNKS
SLOTS = 64
OWN = 4
CAP = 2
REPLICAS = 8
BLOCKS = 128
MESH = pl.DeviceIdType.MESH

decay_rate = 0.9
outer_rate = 0.7
limit_ratio = 0.1


class Place:
    def __init__(self):
        self.replica = lax.axis_index("replica")
        self.shard = lax.axis_index("shard")
        self.y = self.replica // 2
        self.c = self.replica % 2
        self.x = self.shard // 8
        self.z = self.shard % 8
        self.zh = self.z // 4
        self.zl = self.z % 4
        self.self_xy = self.x == self.y
        self.self_z = self.c == self.zh

    def xy_target(self, dx, dc):
        xt = lax.rem(self.x + dx, 4)
        ct = lax.rem(self.c + dc, 2)
        return xt, ct, (2 * self.x + ct, xt * 8 + self.z)

    def xy_source(self, d):
        r = lax.rem(self.replica + d, 8)
        return r, (r, self.y * 8 + self.z)

    def z_target(self, dz):
        zt = lax.rem(self.z + dz, 8)
        return zt, (2 * self.y + self.zh, self.x * 8 + zt)

    def z_source(self, d, dc):
        zs = lax.rem(self.zl + d, 4)
        cs = lax.rem(self.c + dc, 2)
        return zs, cs, (2 * self.y + cs, self.x * 8 + self.c * 4 + zs)

    def shifted(self, dx, dy, dz, dc):
        x = lax.rem(self.x + dx, 4)
        y = lax.rem(self.y + dy, 4)
        z = lax.rem(self.z + dz, 8)
        c = lax.rem(self.c + dc, 2)
        return (y * 2 + c, x * 8 + z)


def columns(half, n):
    return pl.ds(pl.multiple_of(half * HALF + n * DC, 128), DC)


def guarded(maybe_self, condition, act):
    if maybe_self:
        pl.when(jnp.logical_not(condition))(act)
    else:
        act()


def forward_kernel(
    index_ref, coef_ref, deltas_ref, grad_ref, square_ref,
    raw, packed, rx, sums, gx, sq_c, sq_x, sq_y, sq_z,
    load_sem, xy_send, xy_recv, z_send, z_recv, sq_send, sq_recv,
):
    me = Place()
    load = pltpu.make_async_copy(deltas_ref.at[0], raw, load_sem)
    load.start()

    barrier = pltpu.get_barrier_semaphore()

    def greet(device):
        pl.semaphore_signal(barrier, inc=1, device_id=device, device_id_type=MESH)

    for d in range(8):
        guarded(d == 0, me.self_xy, functools.partial(greet, me.xy_source(d)[1]))
    for d in range(4):
        for dc in range(2):
            guarded(d == 0 and dc == 0, me.self_z, functools.partial(greet, me.z_source(d, dc)[2]))
    stages = (
        (sq_c, me.c, [(0, 0, 0, 1)], lambda o: lax.rem(me.c + o[3], 2)),
        (sq_x, me.x, [(d, 0, 0, 0) for d in (1, 2, 3)], lambda o: lax.rem(me.x + o[0], 4)),
        (sq_y, me.y, [(0, d, 0, 0) for d in (1, 2, 3)], lambda o: lax.rem(me.y + o[1], 4)),
        (sq_z, me.z, [(0, 0, d, 0) for d in range(1, 8)], lambda o: lax.rem(me.z + o[2], 8)),
    )
    for _, _, offsets, _ in stages:
        for offset in offsets:
            greet(me.shifted(*offset))

    load.wait()

    def pack(p, carry):
        packed[p] = raw[index_ref[p]]
        return carry

    lax.fori_loop(0, SLOTS, pack, 0)

    pl.semaphore_wait(
        barrier,
        8 + 8 + 14 - me.self_xy.astype(jnp.int32) - me.self_z.astype(jnp.int32),
    )

    def xy_copy(n, dx, dc):
        xt, ct, device = me.xy_target(dx, dc)
        return pltpu.make_async_remote_copy(
            src_ref=packed.at[pl.ds(xt * 16, 16), :, columns(ct, n)],
            dst_ref=rx.at[n, me.replica],
            send_sem=xy_send.at[n, dx * 2 + dc],
            recv_sem=xy_recv.at[n, me.replica],
            device_id=device,
            device_id_type=MESH,
        )

    def xy_arrival(n, d):
        r, device = me.xy_source(d)
        return pltpu.make_async_remote_copy(
            src_ref=packed.at[pl.ds(0, 16), :, columns(0, n)],
            dst_ref=rx.at[n, r],
            send_sem=xy_send.at[n, 0],
            recv_sem=xy_recv.at[n, r],
            device_id=device,
            device_id_type=MESH,
        )

    def z_copy(n, dz):
        zt, device = me.z_target(dz)
        return pltpu.make_async_remote_copy(
            src_ref=sums.at[n, pl.ds(zt * 4, 4)],
            dst_ref=gx.at[n, me.zl * 2 + me.c],
            send_sem=z_send.at[n, dz],
            recv_sem=z_recv.at[n, me.zl * 2 + me.c],
            device_id=device,
            device_id_type=MESH,
        )

    def z_arrival(n, d, dc):
        zs, cs, device = me.z_source(d, dc)
        return pltpu.make_async_remote_copy(
            src_ref=sums.at[n, pl.ds(0, 4)],
            dst_ref=gx.at[n, zs * 2 + cs],
            send_sem=z_send.at[n, 0],
            recv_sem=z_recv.at[n, zs * 2 + cs],
            device_id=device,
            device_id_type=MESH,
        )

    xy_order = [(2, 0), (2, 1), (1, 0), (1, 1), (3, 0), (3, 1), (0, 1), (0, 0)]
    z_order = [4, 3, 5, 2, 6, 1, 7, 0]
    for n in range(CHUNKS):
        for dx, dc in xy_order:
            guarded(dx == 0 and dc == 0, me.self_xy, lambda n=n, dx=dx, dc=dc: xy_copy(n, dx, dc).start())

    @pl.when(me.self_xy)
    def _():
        for n in range(CHUNKS):

            def own(k, carry, n=n):
                rx[n, me.replica, k] = packed[me.x * 16 + k, :, columns(me.c, n)]
                return carry

            lax.fori_loop(0, 16, own, 0)

    total = jnp.zeros((4, DC), jnp.float32)
    for n in range(CHUNKS):
        for d in range(8):
            guarded(d == 0, me.self_xy, lambda n=n, d=d: xy_arrival(n, d).wait_recv())

        def mix(owner, total, n=n):
            acc = [jnp.zeros((4, DC), jnp.float32) for _ in range(OWN)]
            for r in range(REPLICAS):
                for k in range(CAP):
                    rows = rx[n, r, owner * CAP + k].astype(jnp.float32)
                    for j in range(OWN):
                        acc[j] = acc[j] + coef_ref[(r * 16 + owner * CAP + k) * OWN + j] * rows
            for j in range(OWN):
                sums[n, owner * OWN + j] = acc[j]
                total = total + acc[j] * acc[j]
            return total

        total = lax.fori_loop(0, 8, mix, total)
        for dz in z_order:
            guarded(dz == 0, me.self_z, lambda n=n, dz=dz: z_copy(n, dz).start())

        @pl.when(me.self_z)
        def _(n=n):
            for j in range(OWN):
                gx[n, me.zl * 2 + me.c, j] = sums[n, me.z * OWN + j]

    value = jnp.full((8, 128), jnp.sum(total), jnp.float32)
    first = 0
    for slots, mine, offsets, _ in stages:
        slots[mine] = value
        copies = []
        for i, offset in enumerate(offsets):
            copy = pltpu.make_async_remote_copy(
                src_ref=slots.at[mine],
                dst_ref=slots.at[mine],
                send_sem=sq_send.at[first + i],
                recv_sem=sq_recv.at[first + i],
                device_id=me.shifted(*offset),
                device_id_type=MESH,
            )
            copy.start()
            copies.append(copy)
        for copy in copies:
            copy.wait()
        value = slots[0]
        for i in range(1, slots.shape[0]):
            value = value + slots[i]
        first += len(offsets)
    square_ref[...] = value

    for n in range(CHUNKS):
        for d in range(4):
            for dc in range(2):
                guarded(
                    d == 0 and dc == 0, me.self_z, lambda n=n, d=d, dc=dc: z_arrival(n, d, dc).wait_recv()
                )
        for half in range(2):
            for pair in range(2):
                for j in range(OWN):
                    grad_ref[j, pair * 8 : pair * 8 + 8, half * HALF + n * DC : half * HALF + n * DC + DC] = (
                        jnp.concatenate([gx[n, pair * 4 + half, j], gx[n, pair * 4 + 2 + half, j]], axis=0)
                    )

    for n in range(CHUNKS):
        for dx, dc in xy_order:
            guarded(dx == 0 and dc == 0, me.self_xy, lambda n=n, dx=dx, dc=dc: xy_copy(n, dx, dc).wait_send())
        for dz in z_order:
            guarded(dz == 0, me.self_z, lambda n=n, dz=dz: z_copy(n, dz).wait_send())


def forward(index, coef, deltas):
    vmem, dma = pltpu.VMEM, pltpu.SemaphoreType.DMA
    return pl.pallas_call(
        forward_kernel,
        out_shape=(
            jax.ShapeDtypeStruct((OWN, 16, D), jnp.float32),
            jax.ShapeDtypeStruct((8, 128), jnp.float32),
        ),
        in_specs=[
            pl.BlockSpec(memory_space=pltpu.SMEM),
            pl.BlockSpec(memory_space=pltpu.SMEM),
            pl.BlockSpec(memory_space=pl.ANY),
        ],
        out_specs=(pl.BlockSpec(memory_space=vmem), pl.BlockSpec(memory_space=vmem)),
        scratch_shapes=[
            vmem((SLOTS, 4, D), jnp.bfloat16),
            vmem((SLOTS, 4, D), jnp.bfloat16),
            vmem((CHUNKS, REPLICAS, 16, 4, DC), jnp.bfloat16),
            vmem((CHUNKS, 32, 4, DC), jnp.float32),
            vmem((CHUNKS, 8, OWN, 4, DC), jnp.float32),
            vmem((2, 8, 128), jnp.float32),
            vmem((4, 8, 128), jnp.float32),
            vmem((4, 8, 128), jnp.float32),
            vmem((8, 8, 128), jnp.float32),
            dma,
            dma((CHUNKS, 8)),
            dma((CHUNKS, 8)),
            dma((CHUNKS, 8)),
            dma((CHUNKS, 8)),
            dma((14,)),
            dma((14,)),
        ],
        compiler_params=pltpu.CompilerParams(
            collective_id=0, has_side_effects=True, vmem_limit_bytes=40 * 2**20
        ),
        name="forward_exchange",
    )(index, coef, deltas)


def update_kernel(square_ref, grad_ref, params_ref, momentum_ref, new_params_ref, new_momentum_ref, hosted_ref):
    limit = limit_ratio * math.sqrt(BLOCKS * ROWS * D)
    square = square_ref[0:1, 0:1]
    factor = jnp.minimum(1.0, limit / jnp.sqrt(square + 1e-06))
    for j in range(OWN):
        for pair in range(2):
            rows = slice(pair * 8, pair * 8 + 8)
            scaled = factor * grad_ref[j, rows, :]
            new_momentum = decay_rate * momentum_ref[j, rows, :] + scaled
            new_params = params_ref[j, rows, :] - outer_rate * (scaled + decay_rate * new_momentum)
            new_momentum_ref[j, rows, :] = new_momentum
            new_params_ref[j, rows, :] = new_params
            hosted = new_params.astype(jnp.bfloat16)
            hosted_ref[pair * 2, j] = hosted[0:4]
            hosted_ref[pair * 2 + 1, j] = hosted[4:8]


def update(square, grad, params, momentum):
    width = 1024
    wide = pl.BlockSpec((OWN, 16, width), lambda i: (0, 0, i))
    return pl.pallas_call(
        update_kernel,
        grid=(D // width,),
        out_shape=(
            jax.ShapeDtypeStruct((OWN, 16, D), jnp.float32),
            jax.ShapeDtypeStruct((OWN, 16, D), jnp.float32),
            jax.ShapeDtypeStruct((4, OWN, 4, D), jnp.bfloat16),
        ),
        in_specs=[pl.BlockSpec((8, 128), lambda i: (0, 0)), wide, wide, wide],
        out_specs=(wide, wide, pl.BlockSpec((4, OWN, 4, width), lambda i: (0, 0, 0, i))),
        compiler_params=pltpu.CompilerParams(vmem_limit_bytes=40 * 2**20),
        name="outer_update",
    )(square, grad, params, momentum)


def return_kernel(list_ref, hosted_ref, out_ref, *scratch):
    gathered = scratch[0]
    near = scratch[1 : 1 + CHUNKS]
    far = scratch[1 + CHUNKS : 1 + 2 * CHUNKS]
    z_send, z_recv, y_send, y_recv, x_send, x_recv, d_send, d_recv = scratch[1 + 2 * CHUNKS :]
    me = Place()
    sibling = (2 * me.y + 1 - me.c, me.shard)

    barrier = pltpu.get_barrier_semaphore()

    def greet(device):
        pl.semaphore_signal(barrier, inc=1, device_id=device, device_id_type=MESH)

    def z_target(d, dc):
        return me.z_source(d, dc)

    def z_source(dz):
        return me.z_target(dz)

    for dz in range(8):
        guarded(dz == 0, me.self_z, functools.partial(greet, z_source(dz)[1]))
    for d in (1, 2, 3):
        greet(me.shifted(0, d, 0, 0))
        greet(me.shifted(d, 0, 0, 0))
    greet(sibling)
    pl.semaphore_wait(barrier, 8 + 6 + 1 - me.self_z.astype(jnp.int32))

    def z_copy(n, d, dc):
        zt, ct, device = z_target(d, dc)
        return pltpu.make_async_remote_copy(
            src_ref=hosted_ref.at[zt, :, :, columns(ct, n)],
            dst_ref=gathered.at[n, me.y, me.z],
            send_sem=z_send.at[n, d * 2 + dc],
            recv_sem=z_recv.at[n, me.z],
            device_id=device,
            device_id_type=MESH,
        )

    def z_arrival(n, dz):
        zs, device = z_source(dz)
        return pltpu.make_async_remote_copy(
            src_ref=hosted_ref.at[0, :, :, columns(0, n)],
            dst_ref=gathered.at[n, me.y, zs],
            send_sem=z_send.at[n, 0],
            recv_sem=z_recv.at[n, zs],
            device_id=device,
            device_id_type=MESH,
        )

    def y_copy(n, d, arrival=False):
        ys = lax.rem(me.y + d, 4) if arrival else me.y
        return pltpu.make_async_remote_copy(
            src_ref=gathered.at[n, ys],
            dst_ref=gathered.at[n, ys],
            send_sem=y_send.at[n, d],
            recv_sem=y_recv.at[n, ys],
            device_id=me.shifted(0, d, 0, 0),
            device_id_type=MESH,
        )

    def x_copy(n, d):
        return pltpu.make_async_remote_copy(
            src_ref=gathered.at[n, lax.rem(me.x + d, 4)],
            dst_ref=near[n].at[me.x],
            send_sem=x_send.at[n, d],
            recv_sem=x_recv.at[n, me.x],
            device_id=me.shifted(d, 0, 0, 0),
            device_id_type=MESH,
        )

    def x_arrival(n, d):
        xs = lax.rem(me.x + d, 4)
        return pltpu.make_async_remote_copy(
            src_ref=gathered.at[n, xs],
            dst_ref=near[n].at[xs],
            send_sem=x_send.at[n, d],
            recv_sem=x_recv.at[n, xs],
            device_id=me.shifted(d, 0, 0, 0),
            device_id_type=MESH,
        )

    def d_copy(n, d):
        xs = lax.rem(me.x + d, 4)
        return pltpu.make_async_remote_copy(
            src_ref=near[n].at[xs],
            dst_ref=far[n].at[xs],
            send_sem=d_send.at[n, xs],
            recv_sem=d_recv.at[n, xs],
            device_id=sibling,
            device_id_type=MESH,
        )

    z_order = [(d, dc) for d in (2, 1, 3, 0) for dc in (0, 1)]
    order = (2, 1, 3)

    def start_z(n):
        for d, dc in z_order:
            guarded(d == 0 and dc == 0, me.self_z, lambda d=d, dc=dc: z_copy(n, d, dc).start())

        @pl.when(me.self_z)
        def _():
            for j in range(OWN):
                gathered[n, me.y, me.z, j] = hosted_ref[me.zl, j, :, columns(me.c, n)]

    def start_y(n):
        for dz in range(8):
            guarded(dz == 0, me.self_z, lambda dz=dz: z_arrival(n, dz).wait_recv())
        for d in order:
            y_copy(n, d).start()

    def start_x(n):
        for d in order:
            y_copy(n, d, arrival=True).wait_recv()
        for d in order:
            x_copy(n, d).start()

        def own(owner, carry):
            for j in range(OWN):
                near[n][me.x, owner, j] = gathered[n, me.x, owner, j]
            return carry

        lax.fori_loop(0, 8, own, 0)

    def start_d(n):
        d_copy(n, 0).start()
        for d in order:
            x_arrival(n, d).wait_recv()
            d_copy(n, d).start()

    def unpack(n):
        for d in range(4):
            d_copy(n, d).wait_recv()

        def entry(k, carry):
            block = list_ref[me.replica * SLOTS + k]
            safe = jnp.maximum(block, 0)
            for rows, half in ((near[n], me.c), (far[n], 1 - me.c)):
                value = rows[safe // 32, (safe // 4) % 8, safe % 4]
                out_ref[0, k, :, columns(half, n)] = jnp.where(block >= 0, value, jnp.zeros_like(value))
            return carry

        lax.fori_loop(0, SLOTS, entry, 0)

    for n in range(CHUNKS):
        start_z(n)
    for step in range(CHUNKS + 3):
        for lag, stage in enumerate((start_y, start_x, start_d, unpack)):
            if 0 <= step - lag < CHUNKS:
                stage(step - lag)

    for n in range(CHUNKS):
        for d, dc in z_order:
            guarded(d == 0 and dc == 0, me.self_z, lambda n=n, d=d, dc=dc: z_copy(n, d, dc).wait_send())
        for d in order:
            y_copy(n, d).wait_send()
            x_copy(n, d).wait_send()
        for d in range(4):
            d_copy(n, d).wait_send()


def send_back(lists, hosted):
    vmem, dma = pltpu.VMEM, pltpu.SemaphoreType.DMA
    return pl.pallas_call(
        return_kernel,
        out_shape=jax.ShapeDtypeStruct((1, SLOTS, 4, D), jnp.bfloat16),
        in_specs=[pl.BlockSpec(memory_space=pltpu.SMEM), pl.BlockSpec(memory_space=vmem)],
        out_specs=pl.BlockSpec(memory_space=vmem),
        scratch_shapes=[vmem((CHUNKS, 4, 8, OWN, 4, DC), jnp.bfloat16)]
        + [vmem((4, 8, OWN, 4, DC), jnp.bfloat16)] * (2 * CHUNKS)
        + [
            dma((CHUNKS, 8)),
            dma((CHUNKS, 8)),
            dma((CHUNKS, 4)),
            dma((CHUNKS, 4)),
            dma((CHUNKS, 4)),
            dma((CHUNKS, 4)),
            dma((CHUNKS, 4)),
            dma((CHUNKS, 4)),
        ],
        compiler_params=pltpu.CompilerParams(
            collective_id=1, has_side_effects=True, vmem_limit_bytes=40 * 2**20
        ),
        name="return_exchange",
    )(lists, hosted)


def tables(block_list, hosting, counts):
    x = lax.axis_index("shard") // 8
    weight = hosting.reshape(REPLICAS, BLOCKS) * counts
    totals = jnp.maximum(jnp.sum(weight, axis=0).astype(jnp.float32), 1.0)
    ratio = weight.astype(jnp.float32) / totals
    listed = block_list >= 0
    owner = jnp.where(listed, block_list // OWN, -1)
    earlier = jnp.arange(SLOTS)[:, None] < jnp.arange(SLOTS)[None, :]
    same = (owner[:, :, None] == owner[:, None, :]) & earlier[None]
    rank = jnp.sum(same.astype(jnp.int32), axis=1)
    place = jnp.where(listed, owner * CAP + rank, -1)
    my_place = lax.dynamic_index_in_dim(place, lax.axis_index("replica"), 0, keepdims=False)
    found = my_place[None, :] == jnp.arange(SLOTS)[:, None]
    index = jnp.sum(jnp.where(found, jnp.arange(SLOTS)[None, :], 0), axis=1)
    wanted = x * 16 + jnp.arange(16)
    block = jnp.sum(jnp.where(place[:, None, :] == wanted[None, :, None], block_list[:, None, :] + 1, 0), axis=2) - 1
    mine = lax.dynamic_slice_in_dim(ratio, x * 32, 32, 1).reshape(REPLICAS, 8, 1, OWN)
    target = (x * 32 + jnp.arange(32)).reshape(1, 8, 1, OWN)
    coef = jnp.where(block.reshape(REPLICAS, 8, CAP, 1) == target, mine, 0.0)
    return index.astype(jnp.int32), coef.reshape(-1)


def per_device(deltas, block_list, hosting, counts, params, momentum):
    index, coef = tables(block_list, hosting, counts)
    grad, square = forward(index, coef, deltas)
    new_params, new_momentum, hosted = update(square, grad, params, momentum)
    host_params = send_back(block_list.reshape(-1), hosted)
    return new_params, new_momentum, host_params


def solution(mesh):
    blocks = P("shard", "replica", None)
    entries = P("replica", None, "shard", None)
    return jax.shard_map(
        per_device,
        mesh=mesh,
        in_specs=(entries, P(), P(), P(), blocks, blocks),
        out_specs=(blocks, blocks, entries),
        check_vma=False,
    )
```

time: 332 us -> 148 us (0.45)
  the two profiles are of different devices: /device:TPU:1 before, /device:TPU:67 now
where the time goes in v1:
time: 148 us; the launch traced here: 147 us
  Pallas kernels  137 us (93%)
  local copies, waits for them, and re-layouts  5.89 us (4%)
  other arithmetic  3.49 us (2%)
    pallas_call x1, Pallas kernels, send_back(): pl.pallas_call(return_kernel, out_shape=jax.ShapeDtypeStruct((1, SLOTS, 4...  67.6 us
    pallas_call x1, Pallas kernels, forward(): pl.pallas_call(forward_kernel, out_shape=(jax.ShapeDtypeStruct((OWN, 16,...  66.6 us
    unnamed x8, local copies, waits for them, and re-layouts  4.4 us
    pallas_call x1, Pallas kernels, update(): pl.pallas_call(update_kernel, grid=(D // width,), out_shape=(jax.ShapeDty...  3.15 us

profile of v1, /device:TPU:67, one launch (start us, length us, event | category | flops | bytes accessed | tf_op | source)
XLA Modules:
  0.0 147.5 jit_solution(113728960988222694)
XLA Ops:
  0.7 0.8 reshape.64.list_ref
  1.4 0.7 broadcast_add_fusion.1
  2.1 0.1 convert_reduce_fusion
  2.3 0.7 add_select_fusion.1
  3.0 0.3 select_reduce_fusion
  3.3 0.1 select_reduce_fusion.1.index_ref
  3.4 0.1 copy.15
  3.5 0.1 copy.16
  3.6 0.8 copy.17
  4.5 0.1 reshape.63
  4.6 0.7 multiply_reduce_fusion
  5.3 0.7 convert_divide_fusion
  6.0 0.1 constant_dynamic-slice_fusion
  6.0 0.1 copy.18
  6.1 0.1 copy.19
  6.2 0.1 compare_select_fusion
  6.4 0.1 select_n.49.coef_ref
  6.5 0.0 copy-start
  6.5 1.9 %copy-done = bf16[1,64,4,6144]{3,2,1,0:T(4,128)(2,1)S(1)} copy-done((bf16[1,64,4,6144]{3,2,1,0:T(4,128)(2,1)S(1)}, bf16[1,64,4,6144]{3,2,1,0:T(4,128)(2,1)}, u32[]{:S(2)}) %copy-start) | copy-done | bytes 3145752
  8.4 0.0 copy-start.1
  8.4 0.0 copy-start.2
  8.4 66.6 %forward_exchange.1 = (f32[4,16,6144]{2,1,0:T(8,128)S(1)}, f32[8,128]{1,0:T(8,128)S(1)}) custom-call(s32[64]{0:T(128)S(1)} %select_reduce_fusion.1.index_ref, f32[512]{0:T(512)S(1)} %select_n.49.coef_ref, bf16[1,64,4,6144]{3,2,1,0:T(4,128)(2,1)S(1)} %copy-done), custom_call_target="tpu_custom_call" | custom-call | tf_op jit(solution)/shard_map/forward_exchange/pallas_call | solution.py:252
  75.0 0.0 copy-done.1
  75.0 0.0 copy-done.2
  75.1 3.1 %outer_update.1 = (f32[4,16,6144]{2,1,0:T(8,128)}, f32[4,16,6144]{2,1,0:T(8,128)}, bf16[4,4,4,6144]{3,2,1,0:T(4,128)(2,1)S(1)}) custom-call(f32[8,128]{1,0:T(8,128)S(1)} %get-tuple-element.8.square_ref, f32[4,16,6144]{2,1,0:T(8,128)S(1)} %get-tuple-element.9.grad_ref, f32[4,16,6144]{2,1,0:T(8,128)S(1)} %copy-done.1, f32[4,16,6144]{2,1,0:T(8,128)S(1)} %copy-done.2), custom_call_target="tpu_custom_call" | custom-call | tf_op jit(solution)/shard_map/outer_update/pallas_call | solution.py:309
  78.2 67.6 %return_exchange.1 = bf16[1,64,4,6144]{3,2,1,0:T(4,128)(2,1)S(1)} custom-call(s32[512]{0:T(512)S(1)} %reshape.64.list_ref, bf16[4,4,4,6144]{3,2,1,0:T(4,128)(2,1)S(1)} %get-tuple-element.12.hosted_ref), custom_call_target="tpu_custom_call" | custom-call | tf_op jit(solution)/shard_map/return_exchange/pallas_call | solution.py:486
  145.8 1.7 %copy.21 = bf16[1,64,4,6144]{3,2,1,0:T(4,128)(2,1)} copy(bf16[1,64,4,6144]{3,2,1,0:T(4,128)(2,1)S(1)} %return_exchange.1) | data formatting | bytes 6291456
  (6 shorter events, 0.0 us)
Async XLA Ops:
  6.5 1.9 %copy-start = (bf16[1,64,4,6144]{3,2,1,0:T(4,128)(2,1)S(1)}, bf16[1,64,4,6144]{3,2,1,0:T(4,128)(2,1)}, u32[]{:S(2)}) copy-start(bf16[1,64,4,6144]{3,2,1,0:T(4,128)(2,1)} %deltas_ref.1) | copy-start | bytes 9437188
  8.4 66.6 %copy-start.1 = (f32[4,16,6144]{2,1,0:T(8,128)S(1)}, f32[4,16,6144]{2,1,0:T(8,128)}, u32[]{:S(2)}) copy-start(f32[4,16,6144]{2,1,0:T(8,128)} %params_ref.1) | copy-start | bytes 4718596
  8.4 66.6 %copy-start.2 = (f32[4,16,6144]{2,1,0:T(8,128)S(1)}, f32[4,16,6144]{2,1,0:T(8,128)}, u32[]{:S(2)}) copy-start(f32[4,16,6144]{2,1,0:T(8,128)} %momentum_ref.1) | copy-start | bytes 4718596

commit v2 on v1

v2 whole, which is shorter than its diff:
```python
import functools
import math

import jax
import jax.numpy as jnp
from jax import lax
from jax.experimental import pallas as pl
from jax.experimental.pallas import tpu as pltpu
from jax.sharding import PartitionSpec as P

D = 6144
ROWS = 128
HALF = D // 2
CHUNKS = 8
DC = HALF // CHUNKS
SLOTS = 64
OWN = 4
CAP = 2
REPLICAS = 8
BLOCKS = 128
MESH = pl.DeviceIdType.MESH

decay_rate = 0.9
outer_rate = 0.7
limit_ratio = 0.1


class Place:
    def __init__(self):
        self.replica = lax.axis_index("replica")
        self.shard = lax.axis_index("shard")
        self.y = self.replica // 2
        self.c = self.replica % 2
        self.x = self.shard // 8
        self.z = self.shard % 8
        self.zh = self.z // 4
        self.zl = self.z % 4
        self.self_xy = self.x == self.y
        self.self_z = self.c == self.zh

    def xy_target(self, dx, dc):
        xt = lax.rem(self.x + dx, 4)
        ct = lax.rem(self.c + dc, 2)
        return xt, ct, (2 * self.x + ct, xt * 8 + self.z)

    def xy_source(self, d):
        r = lax.rem(self.replica + d, 8)
        return r, (r, self.y * 8 + self.z)

    def z_target(self, dz):
        zt = lax.rem(self.z + dz, 8)
        return zt, (2 * self.y + self.zh, self.x * 8 + zt)

    def z_source(self, d, dc):
        zs = lax.rem(self.zl + d, 4)
        cs = lax.rem(self.c + dc, 2)
        return zs, cs, (2 * self.y + cs, self.x * 8 + self.c * 4 + zs)

    def shifted(self, dx, dy, dz, dc):
        x = lax.rem(self.x + dx, 4)
        y = lax.rem(self.y + dy, 4)
        z = lax.rem(self.z + dz, 8)
        c = lax.rem(self.c + dc, 2)
        return (y * 2 + c, x * 8 + z)


def columns(half, n):
    return pl.ds(pl.multiple_of(half * HALF + n * DC, 128), DC)


def guarded(maybe_self, condition, act):
    if maybe_self:
        pl.when(jnp.logical_not(condition))(act)
    else:
        act()


def exchange_kernel(
    capacity, table_ref, coef_ref, deltas_ref, params_ref, momentum_ref,
    new_params_ref, new_momentum_ref, host_ref, *scratch,
):
    (
        raw, packed, rx, sums, gx, sq_c, sq_x, sq_y, sq_z, params, momentum, new_params, new_momentum,
        hosted, picked, relay, host,
    ) = scratch[:17]
    blocks = scratch[17 : 17 + CHUNKS]
    near = scratch[17 + CHUNKS : 17 + 2 * CHUNKS]
    far = scratch[17 + 2 * CHUNKS : 17 + 3 * CHUNKS]
    (
        load_sem, xy_send, xy_recv, z_send, z_recv, sq_send, sq_recv,
        b_send, b_recv, y_send, y_recv, x_send, x_recv, d_send, d_recv, host_sem,
    ) = scratch[17 + 3 * CHUNKS :]
    me = Place()
    sibling = (2 * me.y + 1 - me.c, me.shard)
    load = pltpu.make_async_copy(deltas_ref.at[0], raw, load_sem.at[0])
    load.start()
    load_params = pltpu.make_async_copy(params_ref, params, load_sem.at[1])
    load_momentum = pltpu.make_async_copy(momentum_ref, momentum, load_sem.at[2])
    load_params.start()
    load_momentum.start()

    barrier = pltpu.get_barrier_semaphore()

    def greet(device):
        pl.semaphore_signal(barrier, inc=1, device_id=device, device_id_type=MESH)

    for d in range(8):
        guarded(d == 0, me.self_xy, functools.partial(greet, me.xy_source(d)[1]))
        guarded(d == 0, me.self_z, functools.partial(greet, me.z_target(d)[1]))
    for d in range(4):
        for dc in range(2):
            guarded(d == 0 and dc == 0, me.self_z, functools.partial(greet, me.z_source(d, dc)[2]))
    stages = (
        (sq_c, me.c, [(0, 0, 0, 1)]),
        (sq_x, me.x, [(d, 0, 0, 0) for d in (1, 2, 3)]),
        (sq_y, me.y, [(0, d, 0, 0) for d in (1, 2, 3)]),
        (sq_z, me.z, [(0, 0, d, 0) for d in range(1, 8)]),
    )
    for _, _, offsets in stages:
        for offset in offsets:
            greet(me.shifted(*offset))

    load.wait()

    def pack(owner, carry):
        for k in range(CAP):
            packed[owner * CAP + k] = raw[table_ref[k, owner]]
        return carry

    lax.fori_loop(0, 32, pack, 0)

    pl.semaphore_wait(
        barrier,
        8 + 16 + 14 - me.self_xy.astype(jnp.int32) - 2 * me.self_z.astype(jnp.int32),
    )

    def xy_copy(n, dx, dc):
        xt, ct, device = me.xy_target(dx, dc)
        return pltpu.make_async_remote_copy(
            src_ref=packed.at[pl.ds(xt * 16, 16), :, columns(ct, n)],
            dst_ref=rx.at[n, me.replica],
            send_sem=xy_send.at[n, dx * 2 + dc],
            recv_sem=xy_recv.at[n, me.replica],
            device_id=device,
            device_id_type=MESH,
        )

    def xy_arrival(n, d):
        r, device = me.xy_source(d)
        return pltpu.make_async_remote_copy(
            src_ref=packed.at[pl.ds(0, 16), :, columns(0, n)],
            dst_ref=rx.at[n, r],
            send_sem=xy_send.at[n, 0],
            recv_sem=xy_recv.at[n, r],
            device_id=device,
            device_id_type=MESH,
        )

    def z_copy(n, dz):
        zt, device = me.z_target(dz)
        return pltpu.make_async_remote_copy(
            src_ref=sums.at[n, pl.ds(zt * 4, 4)],
            dst_ref=gx.at[n, me.zl * 2 + me.c],
            send_sem=z_send.at[n, dz],
            recv_sem=z_recv.at[n, me.zl * 2 + me.c],
            device_id=device,
            device_id_type=MESH,
        )

    def z_arrival(n, d, dc):
        zs, cs, device = me.z_source(d, dc)
        return pltpu.make_async_remote_copy(
            src_ref=sums.at[n, pl.ds(0, 4)],
            dst_ref=gx.at[n, zs * 2 + cs],
            send_sem=z_send.at[n, 0],
            recv_sem=z_recv.at[n, zs * 2 + cs],
            device_id=device,
            device_id_type=MESH,
        )

    xy_order = [(2, 0), (2, 1), (1, 0), (1, 1), (3, 0), (3, 1), (0, 1), (0, 0)]
    z_order = [4, 3, 5, 2, 6, 1, 7, 0]
    for n in range(CHUNKS):
        for dx, dc in xy_order:
            guarded(dx == 0 and dc == 0, me.self_xy, lambda n=n, dx=dx, dc=dc: xy_copy(n, dx, dc).start())

    @pl.when(me.self_xy)
    def _():
        for n in range(CHUNKS):

            def own(k, carry, n=n):
                rx[n, me.replica, k] = packed[me.x * 16 + k, :, columns(me.c, n)]
                return carry

            lax.fori_loop(0, 16, own, 0)

    total = jnp.zeros((4, DC), jnp.float32)
    for n in range(CHUNKS):
        for d in range(8):
            guarded(d == 0, me.self_xy, lambda n=n, d=d: xy_arrival(n, d).wait_recv())

        def mix(owner, total, n=n):
            acc = [jnp.zeros((4, DC), jnp.float32) for _ in range(OWN)]
            for r in range(REPLICAS):
                for k in range(CAP):
                    rows = rx[n, r, owner * CAP + k].astype(jnp.float32)
                    for j in range(OWN):
                        acc[j] = acc[j] + coef_ref[k * REPLICAS + r, me.x * 32 + owner * OWN + j] * rows
            for j in range(OWN):
                sums[n, owner * OWN + j] = acc[j]
                total = total + acc[j] * acc[j]
            return total

        total = lax.fori_loop(0, 8, mix, total)
        for dz in z_order:
            guarded(dz == 0, me.self_z, lambda n=n, dz=dz: z_copy(n, dz).start())

        @pl.when(me.self_z)
        def _(n=n):
            for j in range(OWN):
                gx[n, me.zl * 2 + me.c, j] = sums[n, me.z * OWN + j]

    value = jnp.full((8, 128), jnp.sum(total), jnp.float32)
    first = 0
    for slots, mine, offsets in stages:
        slots[mine] = value
        copies = []
        for i, offset in enumerate(offsets):
            copy = pltpu.make_async_remote_copy(
                src_ref=slots.at[mine],
                dst_ref=slots.at[mine],
                send_sem=sq_send.at[first + i],
                recv_sem=sq_recv.at[first + i],
                device_id=me.shifted(*offset),
                device_id_type=MESH,
            )
            copy.start()
            copies.append(copy)
        for copy in copies:
            copy.wait()
        value = slots[0]
        for i in range(1, slots.shape[0]):
            value = value + slots[i]
        first += len(offsets)

    def b_copy(n, d, dc):
        zt, ct, device = me.z_source(d, dc)
        return pltpu.make_async_remote_copy(
            src_ref=hosted.at[n, ct, zt],
            dst_ref=blocks[n].at[pl.ds(me.z * OWN, OWN)],
            send_sem=b_send.at[n, d * 2 + dc],
            recv_sem=b_recv.at[n, me.z],
            device_id=device,
            device_id_type=MESH,
        )

    def b_arrival(n, dz):
        zs, device = me.z_target(dz)
        return pltpu.make_async_remote_copy(
            src_ref=hosted.at[n, 0, 0],
            dst_ref=blocks[n].at[pl.ds(zs * OWN, OWN)],
            send_sem=b_send.at[n, 0],
            recv_sem=b_recv.at[n, zs],
            device_id=device,
            device_id_type=MESH,
        )

    b_order = [(d, dc) for d in (2, 1, 3, 0) for dc in (0, 1)]
    limit = limit_ratio * math.sqrt(BLOCKS * ROWS * D)
    factor = jnp.minimum(1.0, limit / jnp.sqrt(value + 1e-06))[0:1, 0:1]
    load_params.wait()
    load_momentum.wait()
    for n in range(CHUNKS):
        for d in range(4):
            for dc in range(2):
                guarded(
                    d == 0 and dc == 0, me.self_z, lambda n=n, d=d, dc=dc: z_arrival(n, d, dc).wait_recv()
                )
        for half in range(2):
            wide = slice(half * HALF + n * DC, half * HALF + n * DC + DC)
            for pair in range(2):
                rows = slice(pair * 8, pair * 8 + 8)
                for j in range(OWN):
                    grad = jnp.concatenate([gx[n, pair * 4 + half, j], gx[n, pair * 4 + 2 + half, j]], axis=0)
                    scaled = factor * grad
                    moved = decay_rate * momentum[j, rows, wide] + scaled
                    fresh = params[j, rows, wide] - outer_rate * (scaled + decay_rate * moved)
                    new_momentum[j, rows, wide] = moved
                    new_params[j, rows, wide] = fresh
                    rounded = fresh.astype(jnp.bfloat16)
                    hosted[n, half, pair * 2, j] = rounded[0:4]
                    hosted[n, half, pair * 2 + 1, j] = rounded[4:8]
        for d, dc in b_order:
            guarded(d == 0 and dc == 0, me.self_z, lambda n=n, d=d, dc=dc: b_copy(n, d, dc).start())

        @pl.when(me.self_z)
        def _(n=n):
            for j in range(OWN):
                blocks[n][me.z * OWN + j] = hosted[n, me.c, me.zl, j]

    store_params = pltpu.make_async_copy(new_params, new_params_ref, load_sem.at[1])
    store_momentum = pltpu.make_async_copy(new_momentum, new_momentum_ref, load_sem.at[2])
    store_params.start()
    store_momentum.start()

    def y_copy(n, d, arrival=False):
        ys = lax.rem(me.y + d, 4) if arrival else me.y
        return pltpu.make_async_remote_copy(
            src_ref=picked.at[n, d - 1],
            dst_ref=relay.at[n, ys],
            send_sem=y_send.at[n, d],
            recv_sem=y_recv.at[n, ys],
            device_id=me.shifted(0, d, 0, 0),
            device_id_type=MESH,
        )

    def x_copy(n, d, arrival=False):
        xs = lax.rem(me.x + d, 4)
        xd = xs if arrival else me.x
        return pltpu.make_async_remote_copy(
            src_ref=relay.at[n, xs],
            dst_ref=near[n].at[pl.ds(xd * capacity, capacity)],
            send_sem=x_send.at[n, d],
            recv_sem=x_recv.at[n, xd],
            device_id=me.shifted(d, 0, 0, 0),
            device_id_type=MESH,
        )

    def d_copy(n, d):
        xs = lax.rem(me.x + d, 4)
        return pltpu.make_async_remote_copy(
            src_ref=near[n].at[pl.ds(xs * capacity, capacity)],
            dst_ref=far[n].at[pl.ds(xs * capacity, capacity)],
            send_sem=d_send.at[n, xs],
            recv_sem=d_recv.at[n, xs],
            device_id=sibling,
            device_id_type=MESH,
        )

    def host_copy(n, half):
        return pltpu.make_async_copy(
            host.at[:, :, columns(half, n)], host_ref.at[0, :, :, columns(half, n)], host_sem.at[n, half]
        )

    order = (2, 1, 3)

    def start_y(n):
        for dz in range(8):
            guarded(dz == 0, me.self_z, lambda dz=dz: b_arrival(n, dz).wait_recv())

        def pick(k, carry):
            for d in range(1, 4):
                picked[n, d - 1, k] = blocks[n][table_ref[8 + lax.rem(me.y + d, 4) * 4 + me.x, k]]
            relay[n, me.y, k] = blocks[n][table_ref[8 + me.y * 4 + me.x, k]]
            return carry

        lax.fori_loop(0, capacity, pick, 0)
        for d in order:
            y_copy(n, d).start()

    def start_x(n):
        for d in order:
            y_copy(n, d, arrival=True).wait_recv()
        for d in order:
            x_copy(n, d).start()

        def own(k, carry):
            near[n][me.x * capacity + k] = relay[n, me.x, k]
            return carry

        lax.fori_loop(0, capacity, own, 0)

    def start_d(n):
        d_copy(n, 0).start()
        for d in order:
            x_copy(n, d, arrival=True).wait_recv()
            d_copy(n, d).start()

    def unpack(n):
        for d in range(4):
            d_copy(n, d).wait_recv()

        def entry(k, carry):
            place = table_ref[2, k]
            safe = table_ref[3, k] * capacity + jnp.maximum(place, 0)
            for rows, half in ((near[n], me.c), (far[n], 1 - me.c)):
                value = rows[safe]
                host[k, :, columns(half, n)] = jnp.where(place >= 0, value, jnp.zeros_like(value))
            return carry

        lax.fori_loop(0, SLOTS, entry, 0)
        for half in range(2):
            host_copy(n, half).start()

    for step in range(CHUNKS + 3):
        for lag, stage in enumerate((start_y, start_x, start_d, unpack)):
            if 0 <= step - lag < CHUNKS:
                stage(step - lag)

    for n in range(CHUNKS):
        for dx, dc in xy_order:
            guarded(dx == 0 and dc == 0, me.self_xy, lambda n=n, dx=dx, dc=dc: xy_copy(n, dx, dc).wait_send())
        for dz in z_order:
            guarded(dz == 0, me.self_z, lambda n=n, dz=dz: z_copy(n, dz).wait_send())
        for d, dc in b_order:
            guarded(d == 0 and dc == 0, me.self_z, lambda n=n, d=d, dc=dc: b_copy(n, d, dc).wait_send())
        for d in order:
            y_copy(n, d).wait_send()
            x_copy(n, d).wait_send()
        for d in range(4):
            d_copy(n, d).wait_send()
    store_params.wait()
    store_momentum.wait()
    for n in range(CHUNKS):
        for half in range(2):
            host_copy(n, half).wait()


def exchange(capacity, table, coef, deltas, params, momentum):
    vmem, dma = pltpu.VMEM, pltpu.SemaphoreType.DMA
    smem, anywhere = pl.BlockSpec(memory_space=pltpu.SMEM), pl.BlockSpec(memory_space=pl.ANY)
    owned = jax.ShapeDtypeStruct((OWN, 16, D), jnp.float32)
    return pl.pallas_call(
        functools.partial(exchange_kernel, capacity),
        out_shape=(owned, owned, jax.ShapeDtypeStruct((1, SLOTS, 4, D), jnp.bfloat16)),
        in_specs=[smem, smem, anywhere, anywhere, anywhere],
        out_specs=(anywhere, anywhere, anywhere),
        scratch_shapes=[
            vmem((SLOTS, 4, D), jnp.bfloat16),
            vmem((SLOTS, 4, D), jnp.bfloat16),
            vmem((CHUNKS, REPLICAS, 16, 4, DC), jnp.bfloat16),
            vmem((CHUNKS, 32, 4, DC), jnp.float32),
            vmem((CHUNKS, 8, OWN, 4, DC), jnp.float32),
            vmem((2, 8, 128), jnp.float32),
            vmem((4, 8, 128), jnp.float32),
            vmem((4, 8, 128), jnp.float32),
            vmem((8, 8, 128), jnp.float32),
            vmem((OWN, 16, D), jnp.float32),
            vmem((OWN, 16, D), jnp.float32),
            vmem((OWN, 16, D), jnp.float32),
            vmem((OWN, 16, D), jnp.float32),
            vmem((CHUNKS, 2, 4, OWN, 4, DC), jnp.bfloat16),
            vmem((CHUNKS, 3, capacity, 4, DC), jnp.bfloat16),
            vmem((CHUNKS, 4, capacity, 4, DC), jnp.bfloat16),
            vmem((SLOTS, 4, D), jnp.bfloat16),
        ]
        + [vmem((32, 4, DC), jnp.bfloat16)] * CHUNKS
        + [vmem((4 * capacity, 4, DC), jnp.bfloat16)] * (2 * CHUNKS)
        + [
            dma((3,)),
            dma((CHUNKS, 8)),
            dma((CHUNKS, 8)),
            dma((CHUNKS, 8)),
            dma((CHUNKS, 8)),
            dma((14,)),
            dma((14,)),
            dma((CHUNKS, 8)),
            dma((CHUNKS, 8)),
            dma((CHUNKS, 4)),
            dma((CHUNKS, 4)),
            dma((CHUNKS, 4)),
            dma((CHUNKS, 4)),
            dma((CHUNKS, 4)),
            dma((CHUNKS, 4)),
            dma((CHUNKS, 2)),
        ],
        compiler_params=pltpu.CompilerParams(
            collective_id=capacity, has_side_effects=True, vmem_limit_bytes=56 * 2**20
        ),
        name=f"exchange_{capacity}",
    )(table, coef, deltas, params, momentum)


def tables_kernel(list_ref, hosting_ref, counts_ref, table_ref, coef_ref):
    f32, bf16 = jnp.float32, jnp.bfloat16
    replica = lax.axis_index("replica")

    def iota(shape, axis):
        return lax.broadcasted_iota(jnp.int32, shape, axis)

    def product(left, right, transposed=False):
        return lax.dot_general(
            left.astype(bf16), right.astype(bf16), (((1,), (1 if transposed else 0,)), ((), ())), preferred_element_type=f32
        )

    def as_float(condition):
        return jnp.where(condition, 1.0, 0.0).astype(f32)

    row, col = iota((128, 128), 0), iota((128, 128), 1)
    row8, col8 = iota((8, 128), 0), iota((8, 128), 1)

    def pick_row(array, i):
        return jnp.sum(jnp.where(row8 == i, array, 0.0), axis=0, keepdims=True)

    spread = product(hosting_ref[...].astype(f32), as_float(iota((16, 128), 1) // 8 == iota((16, 128), 0)))
    own_expert = iota((64, 128), 1) % 8 == iota((64, 128), 0) % 8
    hosted = jnp.sum(jnp.where(own_expert, spread, 0.0).reshape(8, 8, 128), axis=1)
    weight = hosted * counts_ref[...].astype(f32)
    totals = jnp.maximum(jnp.sum(weight, axis=0, keepdims=True), 1.0)
    ratio = weight / totals

    entry = iota((8, SLOTS), 1).astype(f32)
    ones_and_entries = jnp.where(iota((8, SLOTS), 0) == 0, 1.0, entry)
    blocks = iota((BLOCKS, SLOTS), 0)

    member = jnp.concatenate(
        [
            product(ones_and_entries, as_float(blocks == list_ref[r : r + 1, :]), transposed=True)[0:1]
            for r in range(REPLICAS)
        ],
        axis=0,
    )
    mine = list_ref[pl.ds(replica, 1), :]
    listed = as_float(blocks == mine)
    entry_of = product(ones_and_entries, listed, transposed=True)[1:2]

    rank = product(member, as_float((row // OWN == col // OWN) & (row < col)))
    coef_ref[0:8, :] = jnp.where(rank < 0.5, ratio, 0.0)
    coef_ref[8:16, :] = jnp.where(rank > 0.5, ratio, 0.0)

    my_rank = pick_row(rank, replica)
    source = entry_of * pick_row(member, replica)
    by_rank = jnp.where((row8 == 0) == (my_rank < 0.5), source, 0.0)
    index = product(by_rank, as_float(row // OWN == col))

    union = jnp.concatenate(
        [jnp.maximum(member[2 * y : 2 * y + 1], member[2 * y + 1 : 2 * y + 2]) for y in range(4)] * 2, axis=0
    )
    place = product(union, as_float((row // 32 == col // 32) & (row < col)))
    my_place = pick_row(place, replica // 2)
    entry_place = product(jnp.broadcast_to(my_place, (8, BLOCKS)), listed)
    most = jnp.max(jnp.where(union > 0.5, place + 1.0, 0.0), keepdims=True)

    table_ref[0:8, :] = index.astype(jnp.int32)
    table_ref[2:3, 0:SLOTS] = jnp.where(mine >= 0, entry_place[0:1].astype(jnp.int32), -1)
    table_ref[3:4, 0:SLOTS] = jnp.maximum(mine, 0) // 32
    table_ref[4:5, :] = jnp.broadcast_to(most.astype(jnp.int32), (1, 128))
    group = jnp.where(col8 // 32 == row8, (col8 % 32).astype(f32), 0.0)
    for y in range(4):
        holds = as_float((place[y : y + 1] == row.astype(f32)) & (union[y : y + 1] > 0.5))
        table_ref[8 + 4 * y : 12 + 4 * y, :] = product(group, holds, transposed=True)[0:4].astype(jnp.int32)


def tables(block_list, hosting, counts):
    return pl.pallas_call(
        tables_kernel,
        out_shape=(jax.ShapeDtypeStruct((24, 128), jnp.int32), jax.ShapeDtypeStruct((16, 128), jnp.float32)),
        name="tables",
    )(block_list, hosting.transpose(0, 2, 1).reshape(64, 16), counts)


def per_device(deltas, block_list, hosting, counts, params, momentum):
    table, coef = tables(block_list, hosting, counts)
    small, full = (functools.partial(exchange, capacity) for capacity in (20, 32))
    return lax.cond(table[4, 0] <= 20, small, full, table, coef, deltas, params, momentum)


def solution(mesh):
    blocks = P("shard", "replica", None)
    entries = P("replica", None, "shard", None)
    return jax.shard_map(
        per_device,
        mesh=mesh,
        in_specs=(entries, P(), P(), P(), blocks, blocks),
        out_specs=(blocks, blocks, entries),
        check_vma=False,
    )
```

time: 148 us -> 121 us (0.82)
  the two profiles are of different devices: /device:TPU:67 before, /device:TPU:1 now
where the time goes in v2:
time: 121 us; the launch traced here: 120 us
  Pallas kernels  112 us (93%)
  local copies, waits for them, and re-layouts  6.11 us (5%)
  between operations  1.3 us (1%)
    pallas_call x1, Pallas kernels, exchange(): pl.pallas_call(functools.partial(exchange_kernel, capacity), out_shape=(o...  111 us
    unnamed x5, local copies, waits for them, and re-layouts  5.59 us

profile of v2, /device:TPU:1, one launch (start us, length us, event | category | flops | bytes accessed | tf_op | source)
XLA Modules:
  0.0 119.5 jit_solution(7000669375601185310)
XLA Ops:
  0.6 1.3 %tables.1 = (s32[24,128]{1,0:T(8,128)S(1)}, f32[16,128]{1,0:T(8,128)S(1)}) custom-call(s32[8,64]{1,0:T(8,128)} %list_ref.1, s32[64,16]{1,0:T(8,128)} %bitcast.4, s32[8,128]{1,0:T(8,128)} %counts_ref.1), custom_call_target="tpu_custom_call" | custom-call | tf_op jit(solution)/shard_map/tables/pallas_call | solution.py:545
  2.0 0.5 slice.3
  3.1 110.8 %conditional.1 = ((f32[4,16,6144]{2,1,0:T(8,128)}, f32[4,16,6144]{2,1,0:T(8,128)}, bf16[1,64,4,6144]{3,2,1,0:T(4,128)(2,1)S(1)})) conditional(s32[]{:T(128)} %bitcast.2, (s32[24,128]{1,0:T(8,128)S(1)}, f32[16,128]{1,0:T(8,128)S(1)}, bf16[1,64,4,6144]{3,2,1,0:T(4,128)(2,1)}, f32[4,16,6144]{2,1,0:T(8,128)}, f32[4,16,6144]{2,1,0:T(8,128)}) %tuple.13, ...), branch_computations={%region_0.0_spmd, %region_1.0_spmd} | conditional | bytes 8 | solution.py:555
  3.2 110.5 %exchange_20.1 = (f32[4,16,6144]{2,1,0:T(8,128)}, f32[4,16,6144]{2,1,0:T(8,128)}, bf16[1,64,4,6144]{3,2,1,0:T(4,128)(2,1)S(1)}) custom-call(s32[24,128]{1,0:T(8,128)S(1)} %get-tuple-element.25.table_ref, f32[16,128]{1,0:T(8,128)S(1)} %get-tuple-element.26.coef_ref, bf16[1,64,4,6144]{3,2,1,0:T(4,128)(2,1)} %get-tuple-element.27.deltas_ref, ...), custom_call_target="tpu_custom_call" | custom-call | tf_op jit(solution)/shard_map/cond/branch_1_fun/exchange_20/pallas_call | solution.py:423
  113.9 0.0 copy-start
  114.0 2.8 %copy.24 = f32[4,16,6144]{2,1,0:T(8,128)} copy(f32[4,16,6144]{2,1,0:T(8,128)} %get-tuple-element.55) | data formatting | bytes 3145728
  116.7 0.0 copy-done
  116.7 1.1 copy.25
  117.9 1.7 %copy.26 = bf16[1,64,4,6144]{3,2,1,0:T(4,128)(2,1)} copy(bf16[1,64,4,6144]{3,2,1,0:T(4,128)(2,1)S(1)} %get-tuple-element.57) | data formatting | bytes 6291456
Async XLA Ops:
  113.9 2.8 %copy-start = (f32[4,16,6144]{2,1,0:T(8,128)S(1)}, f32[4,16,6144]{2,1,0:T(8,128)}, u32[]{:S(2)}) copy-start(f32[4,16,6144]{2,1,0:T(8,128)} %get-tuple-element.56) | copy-start | bytes 4718596

commit v3 on v2

--- a/solution.py
+++ b/solution.py
@@ -12,6 +12,7 @@
 ROWS = 128
 HALF = D // 2
 CHUNKS = 8
+EARLY = 1
 DC = HALF // CHUNKS
 SLOTS = 64
 OWN = 4
@@ -80,22 +81,30 @@
     new_params_ref, new_momentum_ref, host_ref, *scratch,
 ):
     (
-        raw, packed, rx, sums, gx, sq_c, sq_x, sq_y, sq_z, params, momentum, new_params, new_momentum,
-        hosted, picked, relay, host,
-    ) = scratch[:17]
-    blocks = scratch[17 : 17 + CHUNKS]
-    near = scratch[17 + CHUNKS : 17 + 2 * CHUNKS]
-    far = scratch[17 + 2 * CHUNKS : 17 + 3 * CHUNKS]
+        packed, rx, sums, gx, sq_cx, sq_y, sq_z, params, momentum, new_params, new_momentum,
+        kept, base, picked, relay, host,
+    ) = scratch[:16]
+    blocks = scratch[16 : 16 + CHUNKS]
+    near = scratch[16 + CHUNKS : 16 + 2 * CHUNKS]
+    far = scratch[16 + 2 * CHUNKS : 16 + 3 * CHUNKS]
+    raw = scratch[16 + 3 * CHUNKS : 16 + 4 * CHUNKS]
     (
-        load_sem, xy_send, xy_recv, z_send, z_recv, sq_send, sq_recv,
-        b_send, b_recv, y_send, y_recv, x_send, x_recv, d_send, d_recv, host_sem,
-    ) = scratch[17 + 3 * CHUNKS :]
+        load_sem, raw_sem, xy_send, xy_recv, z_send, z_recv, sq_send, sq_recv,
+        a_send, a_recv, y_send, y_recv, x_send, x_recv, d_send, d_recv, host_sem, store_sem,
+    ) = scratch[16 + 4 * CHUNKS :]
     me = Place()
     sibling = (2 * me.y + 1 - me.c, me.shard)
-    load = pltpu.make_async_copy(deltas_ref.at[0], raw, load_sem.at[0])
-    load.start()
-    load_params = pltpu.make_async_copy(params_ref, params, load_sem.at[1])
-    load_momentum = pltpu.make_async_copy(momentum_ref, momentum, load_sem.at[2])
+
+    def raw_copy(n, half):
+        return pltpu.make_async_copy(
+            deltas_ref.at[0, :, :, columns(half, n)], raw[n].at[half], raw_sem.at[n, half]
+        )
+
+    for n in range(CHUNKS):
+        for half in range(2):
+            raw_copy(n, half).start()
+    load_params = pltpu.make_async_copy(params_ref, params, load_sem.at[0])
+    load_momentum = pltpu.make_async_copy(momentum_ref, momentum, load_sem.at[1])
     load_params.start()
     load_momentum.start()
 
@@ -111,8 +120,7 @@
         for dc in range(2):
             guarded(d == 0 and dc == 0, me.self_z, functools.partial(greet, me.z_source(d, dc)[2]))
     stages = (
-        (sq_c, me.c, [(0, 0, 0, 1)]),
-        (sq_x, me.x, [(d, 0, 0, 0) for d in (1, 2, 3)]),
+        (sq_cx, 2 * me.x + me.c, [(d, 0, 0, c) for d in (2, 1, 3, 0) for c in (0, 1) if d or c]),
         (sq_y, me.y, [(0, d, 0, 0) for d in (1, 2, 3)]),
         (sq_z, me.z, [(0, 0, d, 0) for d in range(1, 8)]),
     )
@@ -120,24 +128,29 @@
         for offset in offsets:
             greet(me.shifted(*offset))
 
-    load.wait()
-
-    def pack(owner, carry):
-        for k in range(CAP):
-            packed[owner * CAP + k] = raw[table_ref[k, owner]]
-        return carry
-
-    lax.fori_loop(0, 32, pack, 0)
-
+    def pack(n):
+        for half in range(2):
+            raw_copy(n, half).wait()
+
+        def place(owner, carry):
+            for k in range(CAP):
+                entry = table_ref[k, owner]
+                for half in range(2):
+                    packed[n, half, owner * CAP + k] = raw[n][half, entry]
+            return carry
+
+        lax.fori_loop(0, 32, place, 0)
+
+    pack(0)
     pl.semaphore_wait(
         barrier,
-        8 + 16 + 14 - me.self_xy.astype(jnp.int32) - 2 * me.self_z.astype(jnp.int32),
+        8 + 16 + 17 - me.self_xy.astype(jnp.int32) - 2 * me.self_z.astype(jnp.int32),
     )
 
     def xy_copy(n, dx, dc):
         xt, ct, device = me.xy_target(dx, dc)
         return pltpu.make_async_remote_copy(
-            src_ref=packed.at[pl.ds(xt * 16, 16), :, columns(ct, n)],
+            src_ref=packed.at[n, ct, pl.ds(xt * 16, 16)],
             dst_ref=rx.at[n, me.replica],
             send_sem=xy_send.at[n, dx * 2 + dc],
             recv_sem=xy_recv.at[n, me.replica],
@@ -148,7 +161,7 @@
     def xy_arrival(n, d):
         r, device = me.xy_source(d)
         return pltpu.make_async_remote_copy(
-            src_ref=packed.at[pl.ds(0, 16), :, columns(0, n)],
+            src_ref=packed.at[n, 0, pl.ds(0, 16)],
             dst_ref=rx.at[n, r],
             send_sem=xy_send.at[n, 0],
             recv_sem=xy_recv.at[n, r],
@@ -178,21 +191,68 @@
             device_id_type=MESH,
         )
 
-    xy_order = [(2, 0), (2, 1), (1, 0), (1, 1), (3, 0), (3, 1), (0, 1), (0, 0)]
+    xy_order = [(1, 0), (2, 0), (0, 0), (3, 0), (1, 1), (2, 1), (0, 1), (3, 1)]
     z_order = [4, 3, 5, 2, 6, 1, 7, 0]
+
+    def start_z(n):
+        for dz in z_order:
+            guarded(dz == 0, me.self_z, lambda dz=dz: z_copy(n, dz).start())
+
+    def a_copy(n, d, dc):
+        zt, ct, device = me.z_source(d, dc)
+        return pltpu.make_async_remote_copy(
+            src_ref=kept.at[n, ct, zt],
+            dst_ref=base.at[n, pl.ds(me.z * OWN, OWN)],
+            send_sem=a_send.at[n, d * 2 + dc],
+            recv_sem=a_recv.at[n, me.z],
+            device_id=device,
+            device_id_type=MESH,
+        )
+
+    def a_arrival(n, dz):
+        zs, device = me.z_target(dz)
+        return pltpu.make_async_remote_copy(
+            src_ref=kept.at[n, 0, 0],
+            dst_ref=base.at[n, pl.ds(zs * OWN, OWN)],
+            send_sem=a_send.at[n, 0],
+            recv_sem=a_recv.at[n, zs],
+            device_id=device,
+            device_id_type=MESH,
+        )
+
+    a_order = [(d, dc) for d in (2, 1, 3, 0) for dc in (0, 1)]
     for n in range(CHUNKS):
+        if n > 0:
+            pack(n)
         for dx, dc in xy_order:
             guarded(dx == 0 and dc == 0, me.self_xy, lambda n=n, dx=dx, dc=dc: xy_copy(n, dx, dc).start())
 
-    @pl.when(me.self_xy)
-    def _():
-        for n in range(CHUNKS):
-
-            def own(k, carry, n=n):
-                rx[n, me.replica, k] = packed[me.x * 16 + k, :, columns(me.c, n)]
+        @pl.when(me.self_xy)
+        def _(n=n):
+            def own(k, carry):
+                rx[n, me.replica, k] = packed[n, me.c, me.x * 16 + k]
                 return carry
 
             lax.fori_loop(0, 16, own, 0)
+
+        if n == 0:
+            load_params.wait()
+            load_momentum.wait()
+        for half in range(2):
+            wide = slice(half * HALF + n * DC, half * HALF + n * DC + DC)
+            for pair in range(2):
+                rows = slice(pair * 8, pair * 8 + 8)
+                for j in range(OWN):
+                    keep = params[j, rows, wide] - (outer_rate * decay_rate**2) * momentum[j, rows, wide]
+                    kept[n, half, pair * 2, j] = keep[0:4]
+                    kept[n, half, pair * 2 + 1, j] = keep[4:8]
+        for d, dc in a_order:
+            guarded(d == 0 and dc == 0, me.self_z, lambda n=n, d=d, dc=dc: a_copy(n, d, dc).start())
+
+        @pl.when(me.self_z)
+        def _(n=n):
+            for j in range(OWN):
+                base[n, me.z * OWN + j] = kept[n, me.c, me.zl, j]
 
     total = jnp.zeros((4, DC), jnp.float32)
     for n in range(CHUNKS):
@@ -212,8 +272,8 @@
             return total
 
         total = lax.fori_loop(0, 8, mix, total)
-        for dz in z_order:
-            guarded(dz == 0, me.self_z, lambda n=n, dz=dz: z_copy(n, dz).start())
+        if n < EARLY:
+            start_z(n)
 
         @pl.when(me.self_z)
         def _(n=n):
@@ -236,6 +296,9 @@
             )
             copy.start()
             copies.append(copy)
+        if slots is sq_z:
+            for n in range(EARLY, CHUNKS):
+                start_z(n)
         for copy in copies:
             copy.wait()
         value = slots[0]
@@ -243,39 +306,28 @@
             value = value + slots[i]
         first += len(offsets)
 
-    def b_copy(n, d, dc):
-        zt, ct, device = me.z_source(d, dc)
-        return pltpu.make_async_remote_copy(
-            src_ref=hosted.at[n, ct, zt],
-            dst_ref=blocks[n].at[pl.ds(me.z * OWN, OWN)],
-            send_sem=b_send.at[n, d * 2 + dc],
-            recv_sem=b_recv.at[n, me.z],
-            device_id=device,
-            device_id_type=MESH,
-        )
-
-    def b_arrival(n, dz):
-        zs, device = me.z_target(dz)
-        return pltpu.make_async_remote_copy(
-            src_ref=hosted.at[n, 0, 0],
-            dst_ref=blocks[n].at[pl.ds(zs * OWN, OWN)],
-            send_sem=b_send.at[n, 0],
-            recv_sem=b_recv.at[n, zs],
-            device_id=device,
-            device_id_type=MESH,
-        )
-
-    b_order = [(d, dc) for d in (2, 1, 3, 0) for dc in (0, 1)]
     limit = limit_ratio * math.sqrt(BLOCKS * ROWS * D)
     factor = jnp.minimum(1.0, limit / jnp.sqrt(value + 1e-06))[0:1, 0:1]
-    load_params.wait()
-    load_momentum.wait()
-    for n in range(CHUNKS):
+    step_size = (outer_rate * (1.0 + decay_rate)) * factor
+
+    def store_copies(n):
+        copies = []
+        for half in range(2):
+            wide = slice(half * HALF + n * DC, half * HALF + n * DC + DC)
+            for i, (inside, outside) in enumerate(
+                ((new_params, new_params_ref), (new_momentum, new_momentum_ref))
+            ):
+                copies.append(
+                    pltpu.make_async_copy(
+                        inside.at[:, :, wide], outside.at[:, :, wide], store_sem.at[n, half * 2 + i]
+                    )
+                )
+        return copies
+
+    def update(n):
         for d in range(4):
             for dc in range(2):
-                guarded(
-                    d == 0 and dc == 0, me.self_z, lambda n=n, d=d, dc=dc: z_arrival(n, d, dc).wait_recv()
-                )
+                guarded(d == 0 and dc == 0, me.self_z, lambda d=d, dc=dc: z_arrival(n, d, dc).wait_recv())
         for half in range(2):
             wide = slice(half * HALF + n * DC, half * HALF + n * DC + DC)
             for pair in range(2):
@@ -284,24 +336,10 @@
                     grad = jnp.concatenate([gx[n, pair * 4 + half, j], gx[n, pair * 4 + 2 + half, j]], axis=0)
                     scaled = factor * grad
                     moved = decay_rate * momentum[j, rows, wide] + scaled
-                    fresh = params[j, rows, wide] - outer_rate * (scaled + decay_rate * moved)
                     new_momentum[j, rows, wide] = moved
-                    new_params[j, rows, wide] = fresh
-                    rounded = fresh.astype(jnp.bfloat16)
-                    hosted[n, half, pair * 2, j] = rounded[0:4]
-                    hosted[n, half, pair * 2 + 1, j] = rounded[4:8]
-        for d, dc in b_order:
-            guarded(d == 0 and dc == 0, me.self_z, lambda n=n, d=d, dc=dc: b_copy(n, d, dc).start())
-
-        @pl.when(me.self_z)
-        def _(n=n):
-            for j in range(OWN):
-                blocks[n][me.z * OWN + j] = hosted[n, me.c, me.zl, j]
-
-    store_params = pltpu.make_async_copy(new_params, new_params_ref, load_sem.at[1])
-    store_momentum = pltpu.make_async_copy(new_momentum, new_momentum_ref, load_sem.at[2])
-    store_params.start()
-    store_momentum.start()
+                    new_params[j, rows, wide] = params[j, rows, wide] - outer_rate * (scaled + decay_rate * moved)
+        for copy in store_copies(n):
+            copy.start()
 
     def y_copy(n, d, arrival=False):
         ys = lax.rem(me.y + d, 4) if arrival else me.y
@@ -346,7 +384,13 @@
 
     def start_y(n):
         for dz in range(8):
-            guarded(dz == 0, me.self_z, lambda dz=dz: b_arrival(n, dz).wait_recv())
+            guarded(dz == 0, me.self_z, lambda dz=dz: a_arrival(n, dz).wait_recv())
+
+        def fresh(block, carry):
+            blocks[n][block] = (base[n, block] - step_size * sums[n, block]).astype(jnp.bfloat16)
+            return carry
+
+        lax.fori_loop(0, 32, fresh, 0)
 
         def pick(k, carry):
             for d in range(1, 4):
@@ -392,8 +436,8 @@
         for half in range(2):
             host_copy(n, half).start()
 
-    for step in range(CHUNKS + 3):
-        for lag, stage in enumerate((start_y, start_x, start_d, unpack)):
+    for step in range(CHUNKS + 6):
+        for lag, stage in ((0, start_y), (2, start_x), (4, start_d), (5, unpack), (6, update)):
             if 0 <= step - lag < CHUNKS:
                 stage(step - lag)
 
@@ -402,16 +446,16 @@
             guarded(dx == 0 and dc == 0, me.self_xy, lambda n=n, dx=dx, dc=dc: xy_copy(n, dx, dc).wait_send())
         for dz in z_order:
             guarded(dz == 0, me.self_z, lambda n=n, dz=dz: z_copy(n, dz).wait_send())
-        for d, dc in b_order:
-            guarded(d == 0 and dc == 0, me.self_z, lambda n=n, d=d, dc=dc: b_copy(n, d, dc).wait_send())
+        for d, dc in a_order:
+            guarded(d == 0 and dc == 0, me.self_z, lambda n=n, d=d, dc=dc: a_copy(n, d, dc).wait_send())
         for d in order:
             y_copy(n, d).wait_send()
             x_copy(n, d).wait_send()
         for d in range(4):
             d_copy(n, d).wait_send()
-    store_params.wait()
-    store_momentum.wait()
     for n in range(CHUNKS):
+        for copy in store_copies(n):
+            copy.wait()
         for half in range(2):
             host_copy(n, half).wait()
 
@@ -426,34 +470,35 @@
         in_specs=[smem, smem, anywhere, anywhere, anywhere],
         out_specs=(anywhere, anywhere, anywhere),
         scratch_shapes=[
-            vmem((SLOTS, 4, D), jnp.bfloat16),
-            vmem((SLOTS, 4, D), jnp.bfloat16),
+            vmem((CHUNKS, 2, SLOTS, 4, DC), jnp.bfloat16),
             vmem((CHUNKS, REPLICAS, 16, 4, DC), jnp.bfloat16),
             vmem((CHUNKS, 32, 4, DC), jnp.float32),
             vmem((CHUNKS, 8, OWN, 4, DC), jnp.float32),
-            vmem((2, 8, 128), jnp.float32),
-            vmem((4, 8, 128), jnp.float32),
+            vmem((8, 8, 128), jnp.float32),
             vmem((4, 8, 128), jnp.float32),
             vmem((8, 8, 128), jnp.float32),
             vmem((OWN, 16, D), jnp.float32),
             vmem((OWN, 16, D), jnp.float32),
             vmem((OWN, 16, D), jnp.float32),
             vmem((OWN, 16, D), jnp.float32),
-            vmem((CHUNKS, 2, 4, OWN, 4, DC), jnp.bfloat16),
+            vmem((CHUNKS, 2, 4, OWN, 4, DC), jnp.float32),
+            vmem((CHUNKS, 32, 4, DC), jnp.float32),
             vmem((CHUNKS, 3, capacity, 4, DC), jnp.bfloat16),
             vmem((CHUNKS, 4, capacity, 4, DC), jnp.bfloat16),
             vmem((SLOTS, 4, D), jnp.bfloat16),
         ]
         + [vmem((32, 4, DC), jnp.bfloat16)] * CHUNKS
         + [vmem((4 * capacity, 4, DC), jnp.bfloat16)] * (2 * CHUNKS)
+        + [vmem((2, SLOTS, 4, DC), jnp.bfloat16)] * CHUNKS
         + [
-            dma((3,)),
+            dma((2,)),
+            dma((CHUNKS, 2)),
             dma((CHUNKS, 8)),
             dma((CHUNKS, 8)),
             dma((CHUNKS, 8)),
             dma((CHUNKS, 8)),
-            dma((14,)),
-            dma((14,)),
+            dma((17,)),
+            dma((17,)),
             dma((CHUNKS, 8)),
             dma((CHUNKS, 8)),
             dma((CHUNKS, 4)),
@@ -463,6 +508,7 @@
             dma((CHUNKS, 4)),
             dma((CHUNKS, 4)),
             dma((CHUNKS, 2)),
+            dma((CHUNKS, 4)),
         ],
         compiler_params=pltpu.CompilerParams(
             collective_id=capacity, has_side_effects=True, vmem_limit_bytes=56 * 2**20

time: 121 us -> 110 us (0.909)
  Pallas kernels: 112 us -> 102 us
    pallas_call x1, Pallas kernels: 111 us -> 100 us  [exchange(): pl.pallas_call(functools.partial(exchange_kernel, capacity), out_shape=(o...]
where the time goes in v3:
time: 110 us; the launch traced here: 109 us
  Pallas kernels  102 us (93%)
  local copies, waits for them, and re-layouts  6.11 us (6%)
  between operations  1.3 us (1%)
    pallas_call x1, Pallas kernels, exchange(): pl.pallas_call(functools.partial(exchange_kernel, capacity), out_shape=(o...  100 us
    unnamed x5, local copies, waits for them, and re-layouts  5.59 us

profile of v3, /device:TPU:1, one launch (start us, length us, event | category | flops | bytes accessed | tf_op | source)
XLA Modules:
  0.0 109.5 jit_solution(9682352653407730124)
XLA Ops:
  0.6 1.3 %tables.1 = (s32[24,128]{1,0:T(8,128)S(1)}, f32[16,128]{1,0:T(8,128)S(1)}) custom-call(s32[8,64]{1,0:T(8,128)} %list_ref.1, s32[64,16]{1,0:T(8,128)} %bitcast.4, s32[8,128]{1,0:T(8,128)} %counts_ref.1), custom_call_target="tpu_custom_call" | custom-call | tf_op jit(solution)/shard_map/tables/pallas_call | solution.py:591
  2.0 0.5 slice.3
  3.1 100.7 %conditional.1 = ((f32[4,16,6144]{2,1,0:T(8,128)}, f32[4,16,6144]{2,1,0:T(8,128)}, bf16[1,64,4,6144]{3,2,1,0:T(4,128)(2,1)S(1)})) conditional(s32[]{:T(128)} %bitcast.2, (s32[24,128]{1,0:T(8,128)S(1)}, f32[16,128]{1,0:T(8,128)S(1)}, bf16[1,64,4,6144]{3,2,1,0:T(4,128)(2,1)}, f32[4,16,6144]{2,1,0:T(8,128)}, f32[4,16,6144]{2,1,0:T(8,128)}) %tuple.13, ...), branch_computations={%region_0.0_spmd, %region_1.0_spmd} | conditional | bytes 8 | solution.py:601
  3.2 100.5 %exchange_20.1 = (f32[4,16,6144]{2,1,0:T(8,128)}, f32[4,16,6144]{2,1,0:T(8,128)}, bf16[1,64,4,6144]{3,2,1,0:T(4,128)(2,1)S(1)}) custom-call(s32[24,128]{1,0:T(8,128)S(1)} %get-tuple-element.25.table_ref, f32[16,128]{1,0:T(8,128)S(1)} %get-tuple-element.26.coef_ref, bf16[1,64,4,6144]{3,2,1,0:T(4,128)(2,1)} %get-tuple-element.27.deltas_ref, ...), custom_call_target="tpu_custom_call" | custom-call | tf_op jit(solution)/shard_map/cond/branch_1_fun/exchange_20/pallas_call | solution.py:467
  103.9 0.0 copy-start
  103.9 2.8 %copy.24 = f32[4,16,6144]{2,1,0:T(8,128)} copy(f32[4,16,6144]{2,1,0:T(8,128)} %get-tuple-element.55) | data formatting | bytes 3145728
  106.7 0.0 copy-done
  106.7 1.1 %copy.25 = f32[4,16,6144]{2,1,0:T(8,128)} copy(f32[4,16,6144]{2,1,0:T(8,128)S(1)} %copy-done) | data formatting | bytes 3145728
  107.8 1.7 %copy.26 = bf16[1,64,4,6144]{3,2,1,0:T(4,128)(2,1)} copy(bf16[1,64,4,6144]{3,2,1,0:T(4,128)(2,1)S(1)} %get-tuple-element.57) | data formatting | bytes 6291456
Async XLA Ops:
  103.9 2.8 %copy-start = (f32[4,16,6144]{2,1,0:T(8,128)S(1)}, f32[4,16,6144]{2,1,0:T(8,128)}, u32[]{:S(2)}) copy-start(f32[4,16,6144]{2,1,0:T(8,128)} %get-tuple-element.56) | copy-start | bytes 4718596

commit v4 on v3

--- a/solution.py
+++ b/solution.py
@@ -11,7 +11,7 @@
 D = 6144
 ROWS = 128
 HALF = D // 2
-CHUNKS = 8
+CHUNKS = 6
 EARLY = 1
 DC = HALF // CHUNKS
 SLOTS = 64
@@ -597,8 +597,8 @@
 
 def per_device(deltas, block_list, hosting, counts, params, momentum):
     table, coef = tables(block_list, hosting, counts)
-    small, full = (functools.partial(exchange, capacity) for capacity in (20, 32))
-    return lax.cond(table[4, 0] <= 20, small, full, table, coef, deltas, params, momentum)
+    small, full = (functools.partial(exchange, capacity) for capacity in (18, 32))
+    return lax.cond(table[4, 0] <= 18, small, full, table, coef, deltas, params, momentum)
 
 
 def solution(mesh):

time: 110 us -> 105 us (0.955)
  Pallas kernels: 102 us -> 97.7 us
    pallas_call x1, Pallas kernels: 100 us -> 96.4 us  [exchange(): pl.pallas_call(functools.partial(exchange_kernel, capacity), out_shape=(o...]
where the time goes in v4:
time: 105 us
  Pallas kernels  97.7 us (93%)
  local copies, waits for them, and re-layouts  6.11 us (6%)
  between operations  1.3 us (1%)
    pallas_call x1, Pallas kernels, exchange(): pl.pallas_call(functools.partial(exchange_kernel, capacity), out_shape=(o...  96.4 us
    unnamed x5, local copies, waits for them, and re-layouts  5.59 us

profile of v4, /device:TPU:1, one launch (start us, length us, event | category | flops | bytes accessed | tf_op | source)
XLA Modules:
  0.0 105.1 jit_solution(18421142438899094543)
XLA Ops:
  0.6 1.3 %tables.1 = (s32[24,128]{1,0:T(8,128)S(1)}, f32[16,128]{1,0:T(8,128)S(1)}) custom-call(s32[8,64]{1,0:T(8,128)} %list_ref.1, s32[64,16]{1,0:T(8,128)} %bitcast.4, s32[8,128]{1,0:T(8,128)} %counts_ref.1), custom_call_target="tpu_custom_call" | custom-call | tf_op jit(solution)/shard_map/tables/pallas_call | solution.py:591
  2.0 0.5 slice.3
  3.1 96.4 %conditional.1 = ((f32[4,16,6144]{2,1,0:T(8,128)}, f32[4,16,6144]{2,1,0:T(8,128)}, bf16[1,64,4,6144]{3,2,1,0:T(4,128)(2,1)S(1)})) conditional(s32[]{:T(128)} %bitcast.2, (s32[24,128]{1,0:T(8,128)S(1)}, f32[16,128]{1,0:T(8,128)S(1)}, bf16[1,64,4,6144]{3,2,1,0:T(4,128)(2,1)}, f32[4,16,6144]{2,1,0:T(8,128)}, f32[4,16,6144]{2,1,0:T(8,128)}) %tuple.13, ...), branch_computations={%region_0.0_spmd, %region_1.0_spmd} | conditional | bytes 8 | solution.py:601
  3.2 96.4 %exchange_18.1 = (f32[4,16,6144]{2,1,0:T(8,128)}, f32[4,16,6144]{2,1,0:T(8,128)}, bf16[1,64,4,6144]{3,2,1,0:T(4,128)(2,1)S(1)}) custom-call(s32[24,128]{1,0:T(8,128)S(1)} %get-tuple-element.25.table_ref, f32[16,128]{1,0:T(8,128)S(1)} %get-tuple-element.26.coef_ref, bf16[1,64,4,6144]{3,2,1,0:T(4,128)(2,1)} %get-tuple-element.27.deltas_ref, ...), custom_call_target="tpu_custom_call" | custom-call | tf_op jit(solution)/shard_map/cond/branch_1_fun/exchange_18/pallas_call | solution.py:467
  99.5 0.0 copy-start
  99.5 2.8 %copy.24 = f32[4,16,6144]{2,1,0:T(8,128)} copy(f32[4,16,6144]{2,1,0:T(8,128)} %get-tuple-element.55) | data formatting | bytes 3145728
  102.3 0.0 copy-done
  102.3 1.1 %copy.25 = f32[4,16,6144]{2,1,0:T(8,128)} copy(f32[4,16,6144]{2,1,0:T(8,128)S(1)} %copy-done) | data formatting | bytes 3145728
  103.5 1.7 %copy.26 = bf16[1,64,4,6144]{3,2,1,0:T(4,128)(2,1)} copy(bf16[1,64,4,6144]{3,2,1,0:T(4,128)(2,1)S(1)} %get-tuple-element.57) | data formatting | bytes 6291456
Async XLA Ops:
  99.5 2.8 %copy-start = (f32[4,16,6144]{2,1,0:T(8,128)S(1)}, f32[4,16,6144]{2,1,0:T(8,128)}, u32[]{:S(2)}) copy-start(f32[4,16,6144]{2,1,0:T(8,128)} %get-tuple-element.56) | copy-start | bytes 4718596

commit v5 on v4

--- a/solution.py
+++ b/solution.py
@@ -11,7 +11,7 @@
 D = 6144
 ROWS = 128
 HALF = D // 2
-CHUNKS = 6
+CHUNKS = 4
 EARLY = 1
 DC = HALF // CHUNKS
 SLOTS = 64

time: 105 us -> 107 us (1.019)
  Pallas kernels: 97.7 us -> 99.4 us
    pallas_call x1, Pallas kernels: 96.4 us -> 98.1 us  [exchange(): pl.pallas_call(functools.partial(exchange_kernel, capacity), out_shape=(o...]
where the time goes in v5:
time: 107 us
  Pallas kernels  99.4 us (93%)
  local copies, waits for them, and re-layouts  6.11 us (6%)
  between operations  1.3 us (1%)
    pallas_call x1, Pallas kernels, exchange(): pl.pallas_call(functools.partial(exchange_kernel, capacity), out_shape=(o...  98.1 us
    unnamed x5, local copies, waits for them, and re-layouts  5.59 us

profile of v5, /device:TPU:1, one launch (start us, length us, event | category | flops | bytes accessed | tf_op | source)
XLA Modules:
  0.0 106.9 jit_solution(15279133300975114787)
XLA Ops:
  0.6 1.3 %tables.1 = (s32[24,128]{1,0:T(8,128)S(1)}, f32[16,128]{1,0:T(8,128)S(1)}) custom-call(s32[8,64]{1,0:T(8,128)} %list_ref.1, s32[64,16]{1,0:T(8,128)} %bitcast.4, s32[8,128]{1,0:T(8,128)} %counts_ref.1), custom_call_target="tpu_custom_call" | custom-call | tf_op jit(solution)/shard_map/tables/pallas_call | solution.py:591
  2.0 0.5 slice.3
  3.1 98.1 %conditional.1 = ((f32[4,16,6144]{2,1,0:T(8,128)}, f32[4,16,6144]{2,1,0:T(8,128)}, bf16[1,64,4,6144]{3,2,1,0:T(4,128)(2,1)S(1)})) conditional(s32[]{:T(128)} %bitcast.2, (s32[24,128]{1,0:T(8,128)S(1)}, f32[16,128]{1,0:T(8,128)S(1)}, bf16[1,64,4,6144]{3,2,1,0:T(4,128)(2,1)}, f32[4,16,6144]{2,1,0:T(8,128)}, f32[4,16,6144]{2,1,0:T(8,128)}) %tuple.13, ...), branch_computations={%region_0.0_spmd, %region_1.0_spmd} | conditional | bytes 8 | solution.py:601
  3.2 98.1 %exchange_18.1 = (f32[4,16,6144]{2,1,0:T(8,128)}, f32[4,16,6144]{2,1,0:T(8,128)}, bf16[1,64,4,6144]{3,2,1,0:T(4,128)(2,1)S(1)}) custom-call(s32[24,128]{1,0:T(8,128)S(1)} %get-tuple-element.25.table_ref, f32[16,128]{1,0:T(8,128)S(1)} %get-tuple-element.26.coef_ref, bf16[1,64,4,6144]{3,2,1,0:T(4,128)(2,1)} %get-tuple-element.27.deltas_ref, ...), custom_call_target="tpu_custom_call" | custom-call | tf_op jit(solution)/shard_map/cond/branch_1_fun/exchange_18/pallas_call | solution.py:467
  101.3 0.0 copy-start
  101.3 2.8 %copy.24 = f32[4,16,6144]{2,1,0:T(8,128)} copy(f32[4,16,6144]{2,1,0:T(8,128)} %get-tuple-element.55) | data formatting | bytes 3145728
  104.1 0.0 copy-done
  104.1 1.1 %copy.25 = f32[4,16,6144]{2,1,0:T(8,128)} copy(f32[4,16,6144]{2,1,0:T(8,128)S(1)} %copy-done) | data formatting | bytes 3145728
  105.2 1.7 %copy.26 = bf16[1,64,4,6144]{3,2,1,0:T(4,128)(2,1)} copy(bf16[1,64,4,6144]{3,2,1,0:T(4,128)(2,1)S(1)} %get-tuple-element.57) | data formatting | bytes 6291456
Async XLA Ops:
  101.3 2.8 %copy-start = (f32[4,16,6144]{2,1,0:T(8,128)S(1)}, f32[4,16,6144]{2,1,0:T(8,128)}, u32[]{:S(2)}) copy-start(f32[4,16,6144]{2,1,0:T(8,128)} %get-tuple-element.56) | copy-start | bytes 4718596
